TPU v7x, 512 devices: a whole 4x4x16 slice. The times are simulated.
512 devices in a mesh: utt: 8 (over y, z_hi), tm: 64 (over x, z_lo, core).
Axes of the slice: x: 4, y: 4, z: 16 (z_hi: 2, z_lo: 8; z = z_hi * 8 + z_lo), core: 2. Of those that a mesh axis runs over, the one named last changes fastest.
Arguments:
- stem: bfloat16 [65536, 1280], P(('utt', 'tm')), parts along dimension 0, may hold values from -8 to 8
- norm_gain: float32 [1280], replicated, may hold values from 0.25 to 1.75
- qkv_weight: bfloat16 [1280, 3840], P('tm'), may hold values from -0.2934839 to 0.2934839
- segment_ids: int32 [65536], P(('utt', 'tm')), parts along dimension 0, may hold values from 1 to 21, as said below
- dec_queries: bfloat16 [1024, 1280], P(('utt', 'tm')), parts along dimension 0, may hold values from -9 to 9
- stretch_mask: int32 [1024, 64], P(('utt', 'tm')), parts along dimension 0, may hold values 0 or 1
Outputs:
- memory: bfloat16 [65536, 1280], P(('utt', 'tm')), parts along dimension 0
- cross_out: bfloat16 [1024, 1280], P(('utt', 'tm')), parts along dimension 0
There are 8 independent parts, one for each index of `utt`. A program takes and returns all parts, laid end to end along the dimension named above; an argument that names none is the same for every part. Nothing has to cross between parts.
Inputs may be any that keep to these rules, and one draw needn't show every extreme that they name: `segment_ids`: ids start at 1 and rise by one from run to run; each id covers one contiguous run of at most 512 positions, and the last run is exactly 512 positions long.
All inputs are finite; a program needn't handle non-finite values. No bound on the sum of `stretch_mask` on one device may be relied on, other than what follows from the above.
Results may differ from a plain program's by a relative error of at most 0.0062.
Values may be sent and summed in bfloat16 or wider, within the bound.
A program may use at most 64 MiB of HBM per device.

v0:
```python
import math

import jax
import jax.numpy as jnp
from jax import lax
from jax.sharding import PartitionSpec as P

HD = 64


def from_behind(block, axis, distance):
    devices = range(lax.axis_size(axis))
    route = [(i - distance, i) for i in devices if i - distance in devices]
    return lax.ppermute(block, axis, route)


def on_device(stem, norm_gain, qkv_weight, segment_ids, dec_queries, stretch_mask):
    rows, width = stem.shape
    heads = width // HD
    scale = HD ** (-0.5)
    values_in = stem.astype(jnp.float32)
    mean = jnp.mean(values_in, axis=-1, keepdims=True)
    var = jnp.mean((values_in - mean) ** 2, axis=-1, keepdims=True)
    normed = ((values_in - mean) * lax.rsqrt(var + 1e-05) * norm_gain).astype(jnp.bfloat16)
    projected = jnp.dot(
        normed,
        lax.all_gather(qkv_weight, "tm", axis=0, tiled=True),
        preferred_element_type=jnp.float32,
    ).astype(jnp.bfloat16)
    query_part = projected[:, :width]
    keyvals = projected[:, width:]
    kv_pieces = []
    seg_pieces = []
    for offset in range(-4, 5):
        if offset == 0:
            kv_pieces.append(keyvals)
            seg_pieces.append(segment_ids)
        else:
            kv_pieces.append(from_behind(keyvals, "tm", -offset))
            seg_pieces.append(from_behind(segment_ids, "tm", -offset))
    extended = jnp.concatenate(kv_pieces, axis=0)
    seg_wide = jnp.concatenate(seg_pieces, axis=0)
    same = segment_ids[:, None] == seg_wide[None, :]
    group = math.gcd(heads, 4)
    span = group * HD
    groups = heads // group

    def attend(index):
        start = index * span
        query_group = lax.dynamic_slice_in_dim(query_part, start, span, 1).reshape(rows, group, HD)
        key_group = lax.dynamic_slice_in_dim(extended, start, span, 1).reshape(-1, group, HD)
        value_group = lax.dynamic_slice_in_dim(extended, width + start, span, 1).reshape(
            -1, group, HD
        )
        scores = (
            jnp.einsum("qhd,khd->hqk", query_group, key_group, preferred_element_type=jnp.float32)
            * scale
        )
        scores = jnp.where(same[None], scores, jnp.float32(-1e30))
        top = jnp.max(scores, axis=-1, keepdims=True)
        raised = jnp.exp(scores - top)
        probs = (raised / jnp.sum(raised, axis=-1, keepdims=True)).astype(jnp.bfloat16)
        context = jnp.einsum("hqk,khd->qhd", probs, value_group, preferred_element_type=jnp.float32)
        return context.reshape(rows, span)

    contexts = lax.map(attend, jnp.arange(groups, dtype=jnp.int32))
    context = jnp.transpose(contexts, (1, 0, 2)).reshape(rows, width)
    memory = (values_in + context).astype(jnp.bfloat16)
    tokens_dev = dec_queries.shape[0]
    all_queries = lax.all_gather(dec_queries, "tm", axis=0, tiled=True)
    all_masks = lax.all_gather(stretch_mask, "tm", axis=0, tiled=True)
    total_tokens = all_queries.shape[0]
    device = lax.axis_index("tm")
    column = lax.dynamic_slice_in_dim(all_masks, device, 1, 1)[:, 0]
    owner = jnp.arange(total_tokens, dtype=jnp.int32) // tokens_dev
    allowed = (column == 1) | (owner == device)
    query_heads = all_queries.reshape(total_tokens, heads, HD)
    memory_heads = memory.reshape(rows, heads, HD)
    cross = (
        jnp.einsum("thd,phd->htp", query_heads, memory_heads, preferred_element_type=jnp.float32)
        * scale
    )
    local_top = jnp.max(cross, axis=-1)
    weights = jnp.where(
        allowed[None, :, None], jnp.exp(cross - local_top[:, :, None]), jnp.float32(0.0)
    )
    denom = jnp.transpose(jnp.sum(weights, axis=-1))
    numer = jnp.einsum(
        "htp,phd->thd",
        weights.astype(jnp.bfloat16),
        memory_heads,
        preferred_element_type=jnp.float32,
    )
    top_masked = jnp.transpose(jnp.where(allowed[None, :], local_top, jnp.float32(-1e30)))
    num_all, top_all, den_all = (
        lax.all_to_all(numer[None], "tm", split_axis=1, concat_axis=0, tiled=True),
        lax.all_to_all(top_masked[None], "tm", split_axis=1, concat_axis=0, tiled=True),
        lax.all_to_all(denom[None], "tm", split_axis=1, concat_axis=0, tiled=True),
    )
    best = jnp.max(top_all, axis=0)
    factor = jnp.exp(top_all - best[None])
    num_total = jnp.sum(factor[..., None] * num_all, axis=0)
    den_total = jnp.sum(factor * den_all, axis=0)
    cross_out = (num_total / den_total[..., None]).reshape(tokens_dev, width).astype(jnp.bfloat16)
    return (memory, cross_out)


def solution(mesh):
    placed = (
        P(("utt", "tm"), None),
        P(),
        P("tm", None),
        P(("utt", "tm")),
        P(("utt", "tm"), None),
        P(("utt", "tm"), None),
    )
    return jax.shard_map(
        on_device,
        mesh=mesh,
        in_specs=placed,
        out_specs=(P(("utt", "tm"), None), P(("utt", "tm"), None)),
        check_vma=False,
    )
```

profile of v0, /device:TPU:1, one launch (start us, length us, event | category | flops | bytes accessed | tf_op | source)
XLA Modules:
  0.0 600.4 jit_solution(3820719611877599102)
XLA Ops:
  7.9 1.3 collective-permute-start.14
  9.2 1.3 collective-permute-start.13
  10.5 8.7 %collective-permute-start.12 = (s32[128]{0:T(128)}, s32[128]{0:T(128)S(1)}, u32[]{:S(2)}, u32[]{:S(2)}) collective-permute-start(s32[128]{0:T(128)} %param.11), channel_id=1, source_target_pairs={{1,0},{2,1},{3,2},{4,3},{5,4},{6,5},{7,6},{8,7},{9,8},{10,9},{11,1... | collective-permute-start | bytes 1544 | tf_op jit(solution)/shard_map/ppermute | solution.py:14
  19.3 4.2 collective-permute-start.11
  23.4 5.2 collective-permute-start.8
  28.6 116.4 %all-gather.1 = s32[64,2,64]{2,1,0:T(2,128)S(1)} all-gather(s32[1,2,64]{2,1,0:T(2,128)} %bitcast.74), channel_id=1, replica_groups=mesh['utt'=8,'tm'=64] {'tm'}, dimensions={0}, use_global_device_ids=true | all-gather | bytes 33280 | tf_op jit(solution)/shard_map/all_gather | solution.py:71
  145.1 1.2 copy.39
  146.7 114.0 %all-gather.2 = bf16[64,2,1280]{2,1,0:T(2,128)(2,1)S(1)} all-gather(bf16[1,2,1280]{2,1,0:T(2,128)(2,1)} %bitcast.73), channel_id=1, replica_groups=mesh['utt'=8,'tm'=64] {'tm'}, dimensions={0}, use_global_device_ids=true | all-gather | bytes 332800 | tf_op jit(solution)/shard_map/all_gather | solution.py:70
  261.4 1.3 collective-permute-start.9
  263.4 6.1 %collective-permute-start.10 = (s32[128]{0:T(128)S(1)}, s32[128]{0:T(128)S(1)}, u32[]{:S(2)}, u32[]{:S(2)}) collective-permute-start(s32[128]{0:T(128)S(1)} %copy-done.1), channel_id=1, source_target_pairs={{0,2},{1,3},{2,4},{3,5},{4,6},{5,7},{6,8},{7,9},{8,10},{9,11},{10,... | collective-permute-start | bytes 1544 | tf_op jit(solution)/shard_map/ppermute | solution.py:14
  270.2 1.3 collective-permute-start.15
  271.5 13.7 %reshape.128 = bf16[1280,3840]{1,0:T(8,128)(2,1)} reshape(bf16[64,20,3840]{2,1,0:T(8,128)(2,1)} %all-gather.5.cloned.1.call-done) | data formatting | bytes 19660800
  285.2 5.3 convolution_convert_fusion
  290.6 4.9 collective-permute-start
  295.6 5.5 collective-permute-start.1
  301.2 1.3 collective-permute-start.7
  302.5 1.3 collective-permute-start.6
  303.8 1.3 collective-permute-start.5
  305.1 4.9 collective-permute-done
  310.0 24.2 %collective-permute-start.2 = (bf16[128,2560]{1,0:T(8,128)(2,1)S(1)}, bf16[128,2560]{1,0:T(8,128)(2,1)S(1)}, u32[]{:S(2)}, u32[]{:S(2)}) collective-permute-start(bf16[128,2560]{1,0:T(8,128)(2,1)S(1)} %slice.8), channel_id=1, source_target_pairs={{0,2},{1,3},{2,4},{3,5},{4,6},{5,7},{6,8},{7,9},{8,10},{9,11},{10,... | collective-permute-start | bytes 1966088 | tf_op jit(solution)/shard_map/ppermute | solution.py:14
  334.2 0.9 constant_dynamic-update-slice_fusion.9
  335.1 13.4 %collective-permute-start.3 = (bf16[128,2560]{1,0:T(8,128)(2,1)S(1)}, bf16[128,2560]{1,0:T(8,128)(2,1)S(1)}, u32[]{:S(2)}, u32[]{:S(2)}) collective-permute-start(bf16[128,2560]{1,0:T(8,128)(2,1)S(1)} %slice.8), channel_id=1, source_target_pairs={{0,1},{1,2},{2,3},{3,4},{4,5},{5,6},{6,7},{7,8},{8,9},{9,10},{10,1... | collective-permute-start | bytes 1966088 | tf_op jit(solution)/shard_map/ppermute | solution.py:14
  348.6 0.9 constant_dynamic-update-slice_fusion.8
  349.5 1.9 collective-permute-start.4
  352.2 3.8 collective-permute-done.3
  356.1 0.9 constant_dynamic-update-slice_fusion.6
  357.0 0.9 constant_dynamic-update-slice_fusion.5
  357.9 53.3 %collective-permute-done.4 = bf16[128,2560]{1,0:T(8,128)(2,1)S(1)} collective-permute-done((bf16[128,2560]{1,0:T(8,128)(2,1)S(1)}, bf16[128,2560]{1,0:T(8,128)(2,1)S(1)}, u32[]{:S(2)}, u32[]{:S(2)}) %collective-permute-start.4) | collective-permute-done | bytes 655392 | tf_op jit(solution)/shard_map/ppermute | solution.py:14
  411.2 0.9 constant_dynamic-update-slice_fusion.4
  413.0 11.1 %collective-permute-done.6 = bf16[128,2560]{1,0:T(8,128)(2,1)S(1)} collective-permute-done((bf16[128,2560]{1,0:T(8,128)(2,1)S(1)}, bf16[128,2560]{1,0:T(8,128)(2,1)S(1)}, u32[]{:S(2)}, u32[]{:S(2)}) %collective-permute-start.6) | collective-permute-done | bytes 655392 | tf_op jit(solution)/shard_map/ppermute | solution.py:14
  424.1 0.9 constant_dynamic-update-slice_fusion.2
  425.0 0.9 constant_dynamic-update-slice_fusion.1
  425.9 8.9 %copy.40 = bf16[1152,2560]{0,1:T(8,128)(2,1)} copy(bf16[1152,2560]{1,0:T(8,128)(2,1)} %constant_dynamic-update-slice_fusion.1) | data formatting | bytes 11796480
  434.8 41.2 %while.13 = (s32[]{:T(128)}, f32[5,128,256]{1,2,0:T(8,128)}, s32[5]{0:T(128)S(1)}, bf16[1152,2560]{0,1:T(8,128)(2,1)}, bf16[128,1280]{1,0:T(8,128)(2,1)S(1)}, /*...) while((s32[]{:T(128)}, f32[5,128,256]{1,2,0:T(8,128)}, ...), condition=%wide.region_5.6_spmd.clone, body=%wide.region_2.5_spmd.clone.sunk | while | flops 154682496 | bytes 9282826 | solution.py:66
  436.3 1.3 constant_dynamic-slice_fusion.5
  437.7 2.4 fusion.45
  440.1 2.3 fusion.46
  444.6 1.3 constant_dynamic-slice_fusion.5
  445.9 2.4 fusion.45
  448.3 2.3 fusion.46
  452.8 1.3 constant_dynamic-slice_fusion.5
  454.2 2.4 fusion.45
  456.5 2.3 fusion.46
  461.1 1.3 constant_dynamic-slice_fusion.5
  462.4 2.4 fusion.45
  464.8 2.3 fusion.46
  469.3 1.3 constant_dynamic-slice_fusion.5
  470.6 2.4 fusion.45
  473.0 2.3 fusion.46
  476.0 1.2 fusion.18
  478.7 32.9 %all-to-all-start.2 = ((f32[1,128,20]{2,0,1:T(1,128)}), f32[1,128,20]{2,0,1:T(1,128)S(1)}, u32[]{:S(2)}, u32[]{:S(2)}) async-start(f32[1,128,20]{2,0,1:T(1,128)} %copy.49), calls=%async_computation.2 | async-start | bytes 131072 | tf_op jit(solution)/shard_map/all_to_all | solution.py:98
  512.4 12.1 %all-to-all-done.2 = f32[1,128,20]{2,0,1:T(1,128)S(1)} async-done(((f32[1,128,20]{2,0,1:T(1,128)}), f32[1,128,20]{2,0,1:T(1,128)S(1)}, u32[]{:S(2)}, u32[]{:S(2)}) %all-to-all-start.2) | async-done | bytes 10272 | tf_op jit(solution)/shard_map/all_to_all | solution.py:98
  524.5 5.0 all-to-all-start
  529.5 1.2 convolution_bitcast_fusion
  530.7 2.5 copy.47
  533.7 3.9 reduce
  537.6 1.7 reshape.137
  539.3 3.0 all-to-all-done
  542.3 10.1 %all-to-all-start.1 = ((f32[64,1,2560]{2,1,0:T(1,128)}), f32[64,1,2560]{2,1,0:T(1,128)S(1)}, u32[]{:S(2)}, u32[]{:S(2)}) async-start(f32[64,1,2560]{2,1,0:T(1,128)} %reshape.137), calls=%async_computation.1 | async-start | bytes 1310720 | tf_op jit(solution)/shard_map/all_to_all | solution.py:96
  552.4 0.9 copy.52
  554.3 32.7 %all-to-all-done.1 = f32[64,1,2560]{2,1,0:T(1,128)S(1)} async-done(((f32[64,1,2560]{2,1,0:T(1,128)}), f32[64,1,2560]{2,1,0:T(1,128)S(1)}, u32[]{:S(2)}, u32[]{:S(2)}) %all-to-all-start.1) | async-done | bytes 655392 | tf_op jit(solution)/shard_map/all_to_all | solution.py:96
  587.0 2.2 reduce.1
  589.3 1.6 reshape.138
  591.0 1.7 multiply_reduce_fusion
  (85 shorter events, 17.5 us)
Async XLA Ops:
  7.2 254.2 %copy-start.1 = (s32[128]{0:T(128)S(1)}, s32[128]{0:T(128)}, u32[]{:S(2)}) copy-start(s32[128]{0:T(128)} %param.11) | copy-start | bytes 1540
  7.2 264.3 %all-gather.5.cloned.1.call-start = ((), (), s32[]{:S(2)}) async-start(), calls=%async_computation.3 | async-start | bytes 11980800 | tf_op jit(solution)/shard_map/all_gather | solution.py:27
  7.9 293.2 %collective-permute-start.14 = (s32[128]{0:T(128)}, s32[128]{0:T(128)S(1)}, u32[]{:S(2)}, u32[]{:S(2)}) collective-permute-start(s32[128]{0:T(128)} %param.11), channel_id=1, source_target_pairs={{3,0},{4,1},{5,2},{6,3},{7,4},{8,5},{9,6},{10,7},{11,8},{12,9},{13... | collective-permute-start | bytes 1544 | tf_op jit(solution)/shard_map/ppermute | solution.py:14
  9.2 291.9 %collective-permute-start.13 = (s32[128]{0:T(128)}, s32[128]{0:T(128)S(1)}, u32[]{:S(2)}, u32[]{:S(2)}) collective-permute-start(s32[128]{0:T(128)} %param.11), channel_id=1, source_target_pairs={{2,0},{3,1},{4,2},{5,3},{6,4},{7,5},{8,6},{9,7},{10,8},{11,9},{12,... | collective-permute-start | bytes 1544 | tf_op jit(solution)/shard_map/ppermute | solution.py:14
  10.5 285.0 %collective-permute-start.12 = (s32[128]{0:T(128)}, s32[128]{0:T(128)S(1)}, u32[]{:S(2)}, u32[]{:S(2)}) collective-permute-start(s32[128]{0:T(128)} %param.11), channel_id=1, source_target_pairs={{1,0},{2,1},{3,2},{4,3},{5,4},{6,5},{7,6},{8,7},{9,8},{10,9},{11,1... | collective-permute-start | bytes 1544 | tf_op jit(solution)/shard_map/ppermute | solution.py:14
  19.3 271.3 %collective-permute-start.11 = (s32[128]{0:T(128)}, s32[128]{0:T(128)S(1)}, u32[]{:S(2)}, u32[]{:S(2)}) collective-permute-start(s32[128]{0:T(128)} %param.11), channel_id=1, source_target_pairs={{0,1},{1,2},{2,3},{3,4},{4,5},{5,6},{6,7},{7,8},{8,9},{9,10},{10,1... | collective-permute-start | bytes 1544 | tf_op jit(solution)/shard_map/ppermute | solution.py:14
  23.4 237.9 %collective-permute-start.8 = (s32[128]{0:T(128)}, s32[128]{0:T(128)S(1)}, u32[]{:S(2)}, u32[]{:S(2)}) collective-permute-start(s32[128]{0:T(128)} %param.11), channel_id=1, source_target_pairs={{0,4},{1,5},{2,6},{3,7},{4,8},{5,9},{6,10},{7,11},{8,12},{9,13},{1... | collective-permute-start | bytes 1544 | tf_op jit(solution)/shard_map/ppermute | solution.py:14
  261.4 2.0 collective-permute-start.9
  263.4 6.8 %collective-permute-start.10 = (s32[128]{0:T(128)S(1)}, s32[128]{0:T(128)S(1)}, u32[]{:S(2)}, u32[]{:S(2)}) collective-permute-start(s32[128]{0:T(128)S(1)} %copy-done.1), channel_id=1, source_target_pairs={{0,2},{1,3},{2,4},{3,5},{4,6},{5,7},{6,8},{7,9},{8,10},{9,11},{10,... | collective-permute-start | bytes 1544 | tf_op jit(solution)/shard_map/ppermute | solution.py:14
  270.2 31.0 %collective-permute-start.15 = (s32[128]{0:T(128)S(1)}, s32[128]{0:T(128)S(1)}, u32[]{:S(2)}, u32[]{:S(2)}) collective-permute-start(s32[128]{0:T(128)S(1)} %copy-done.1), channel_id=1, source_target_pairs={{4,0},{5,1},{6,2},{7,3},{8,4},{9,5},{10,6},{11,7},{12,8},{13,9},{1... | collective-permute-start | bytes 1544 | tf_op jit(solution)/shard_map/ppermute | solution.py:14
  271.5 13.7 %copy-start.2 = (f32[1280]{0:T(1024)S(1)}, f32[1280]{0:T(1024)}, u32[]{:S(2)}) copy-start(f32[1280]{0:T(1024)} %param.9) | copy-start | bytes 15364
  290.5 66.5 %copy-start = (bf16[128,3840]{1,0:T(8,128)(2,1)}, bf16[128,3840]{1,0:T(8,128)(2,1)S(1)}, u32[]{:S(2)}) copy-start(bf16[128,3840]{1,0:T(8,128)(2,1)S(1)} %convolution_convert_fusion) | copy-start | bytes 2949124
  290.6 19.4 %collective-permute-start = (bf16[128,2560]{1,0:T(8,128)(2,1)S(1)}, bf16[128,2560]{1,0:T(8,128)(2,1)S(1)}, u32[]{:S(2)}, u32[]{:S(2)}) collective-permute-start(bf16[128,2560]{1,0:T(8,128)(2,1)S(1)} %slice.8), channel_id=1, source_target_pairs={{0,4},{1,5},{2,6},{3,7},{4,8},{5,9},{6,10},{7,11},{8,12},{9,13},{1... | collective-permute-start | bytes 1966088 | tf_op jit(solution)/shard_map/ppermute | solution.py:14
  295.6 39.6 %collective-permute-start.1 = (bf16[128,2560]{1,0:T(8,128)(2,1)S(1)}, bf16[128,2560]{1,0:T(8,128)(2,1)S(1)}, u32[]{:S(2)}, u32[]{:S(2)}) collective-permute-start(bf16[128,2560]{1,0:T(8,128)(2,1)S(1)} %slice.8), channel_id=1, source_target_pairs={{0,3},{1,4},{2,5},{3,6},{4,7},{5,8},{6,9},{7,10},{8,11},{9,12},{10... | collective-permute-start | bytes 1966088 | tf_op jit(solution)/shard_map/ppermute | solution.py:14
  301.2 123.8 %collective-permute-start.7 = (bf16[128,2560]{1,0:T(8,128)(2,1)S(1)}, bf16[128,2560]{1,0:T(8,128)(2,1)S(1)}, u32[]{:S(2)}, u32[]{:S(2)}) collective-permute-start(bf16[128,2560]{1,0:T(8,128)(2,1)S(1)} %slice.8), channel_id=1, source_target_pairs={{4,0},{5,1},{6,2},{7,3},{8,4},{9,5},{10,6},{11,7},{12,8},{13,9},{1... | collective-permute-start | bytes 1966088 | tf_op jit(solution)/shard_map/ppermute | solution.py:14
  302.5 121.6 %collective-permute-start.6 = (bf16[128,2560]{1,0:T(8,128)(2,1)S(1)}, bf16[128,2560]{1,0:T(8,128)(2,1)S(1)}, u32[]{:S(2)}, u32[]{:S(2)}) collective-permute-start(bf16[128,2560]{1,0:T(8,128)(2,1)S(1)} %slice.8), channel_id=1, source_target_pairs={{3,0},{4,1},{5,2},{6,3},{7,4},{8,5},{9,6},{10,7},{11,8},{12,9},{13... | collective-permute-start | bytes 1966088 | tf_op jit(solution)/shard_map/ppermute | solution.py:14
  303.8 108.4 %collective-permute-start.5 = (bf16[128,2560]{1,0:T(8,128)(2,1)S(1)}, bf16[128,2560]{1,0:T(8,128)(2,1)S(1)}, u32[]{:S(2)}, u32[]{:S(2)}) collective-permute-start(bf16[128,2560]{1,0:T(8,128)(2,1)S(1)} %slice.8), channel_id=1, source_target_pairs={{2,0},{3,1},{4,2},{5,3},{6,4},{7,5},{8,6},{9,7},{10,8},{11,9},{12,... | collective-permute-start | bytes 1966088 | tf_op jit(solution)/shard_map/ppermute | solution.py:14
  310.0 39.5 %collective-permute-start.2 = (bf16[128,2560]{1,0:T(8,128)(2,1)S(1)}, bf16[128,2560]{1,0:T(8,128)(2,1)S(1)}, u32[]{:S(2)}, u32[]{:S(2)}) collective-permute-start(bf16[128,2560]{1,0:T(8,128)(2,1)S(1)} %slice.8), channel_id=1, source_target_pairs={{0,2},{1,3},{2,4},{3,5},{4,6},{5,7},{6,8},{7,9},{8,10},{9,11},{10,... | collective-permute-start | bytes 1966088 | tf_op jit(solution)/shard_map/ppermute | solution.py:14
  335.1 20.9 %collective-permute-start.3 = (bf16[128,2560]{1,0:T(8,128)(2,1)S(1)}, bf16[128,2560]{1,0:T(8,128)(2,1)S(1)}, u32[]{:S(2)}, u32[]{:S(2)}) collective-permute-start(bf16[128,2560]{1,0:T(8,128)(2,1)S(1)} %slice.8), channel_id=1, source_target_pairs={{0,1},{1,2},{2,3},{3,4},{4,5},{5,6},{6,7},{7,8},{8,9},{9,10},{10,1... | collective-permute-start | bytes 1966088 | tf_op jit(solution)/shard_map/ppermute | solution.py:14
  349.5 61.8 %collective-permute-start.4 = (bf16[128,2560]{1,0:T(8,128)(2,1)S(1)}, bf16[128,2560]{1,0:T(8,128)(2,1)S(1)}, u32[]{:S(2)}, u32[]{:S(2)}) collective-permute-start(bf16[128,2560]{1,0:T(8,128)(2,1)S(1)} %slice.8), channel_id=1, source_target_pairs={{1,0},{2,1},{3,2},{4,3},{5,4},{6,5},{7,6},{8,7},{9,8},{10,9},{11,1... | collective-permute-start | bytes 1966088 | tf_op jit(solution)/shard_map/ppermute | solution.py:14
  425.9 8.9 %slice-start = ((bf16[128,3840]{1,0:T(8,128)(2,1)}), bf16[128,1280]{1,0:T(8,128)(2,1)S(1)}, s32[]{:S(2)}) async-start(bf16[128,3840]{1,0:T(8,128)(2,1)} %copy-done), calls=%async_computation.4 | async-start | bytes 655360 | tf_op jit(solution)/shard_map/slice | solution.py:30
  478.7 45.7 %all-to-all-start.2 = ((f32[1,128,20]{2,0,1:T(1,128)}), f32[1,128,20]{2,0,1:T(1,128)S(1)}, u32[]{:S(2)}, u32[]{:S(2)}) async-start(f32[1,128,20]{2,0,1:T(1,128)} %copy.49), calls=%async_computation.2 | async-start | bytes 131072 | tf_op jit(solution)/shard_map/all_to_all | solution.py:98
  524.5 17.8 %all-to-all-start = ((f32[1,128,20]{2,0,1:T(1,128)}), f32[1,128,20]{2,0,1:T(1,128)S(1)}, u32[]{:S(2)}, u32[]{:S(2)}) async-start(f32[1,128,20]{2,0,1:T(1,128)} %copy.44), calls=%async_computation | async-start | bytes 131072 | tf_op jit(solution)/shard_map/all_to_all | solution.py:97
  542.3 44.7 %all-to-all-start.1 = ((f32[64,1,2560]{2,1,0:T(1,128)}), f32[64,1,2560]{2,1,0:T(1,128)S(1)}, u32[]{:S(2)}, u32[]{:S(2)}) async-start(f32[64,1,2560]{2,1,0:T(1,128)} %reshape.137), calls=%async_computation.1 | async-start | bytes 1310720 | tf_op jit(solution)/shard_map/all_to_all | solution.py:96
Sparse Core Ops, SparseCore 0:
  10.1 136.0 all-gather.4
where the time goes:
time: 602 us; the launch traced here: 600 us
  blocking collectives  230 us (38%)
  starting transfers between devices  131 us (22%)
  waiting for transfers between devices  123 us (20%)
  local copies, waits for them, and re-layouts  56.6 us (9%)
  matrix products  30.5 us (5%)
  between operations  14.5 us (2%)
  other arithmetic  10.7 us (2%)
    all_gather x1, blocking collectives, on_device(): all_masks = lax.all_gather(stretch_mask, 'tm', axis=0, tiled=True)  116 us
    all_gather x1, blocking collectives, on_device(): all_queries = lax.all_gather(dec_queries, 'tm', axis=0, tiled=True)  114 us
    ppermute x16, starting transfers between devices, from_behind(): return lax.ppermute(block, axis, route)  83.2 us
    ppermute x16, waiting for transfers between devices, from_behind(): return lax.ppermute(block, axis, route)  74.5 us
    unnamed x30, local copies, waits for them, and re-layouts  35.9 us
    all_to_all x1, starting transfers between devices, on_device(): lax.all_to_all(denom[None], 'tm', split_axis=1, concat_axis=0, tiled=True)  32.9 us
    all_to_all x1, waiting for transfers between devices, on_device(): lax.all_to_all(numer[None], 'tm', split_axis=1, concat_axis=0, tiled=True)  32.7 us
    all_to_all x1, waiting for transfers between devices, on_device(): lax.all_to_all(denom[None], 'tm', split_axis=1, concat_axis=0, tiled=True)  12.1 us
  transfers between devices with their start and end apart: 20, of which 9 were waited for; matrix products, arithmetic and copies ran while one was open for 7% of the time, Pallas kernels for 0%

commit v1 on v0

--- a/solution.py
+++ b/solution.py
@@ -18,28 +18,48 @@
     rows, width = stem.shape
     heads = width // HD
     scale = HD ** (-0.5)
+    tokens_dev = dec_queries.shape[0]
+    n_tm = lax.axis_size("tm")
+    device = lax.axis_index("tm")
+    small = jnp.concatenate(
+        [
+            dec_queries.reshape(-1),
+            stretch_mask.astype(jnp.bfloat16).reshape(-1),
+            (segment_ids % 128).astype(jnp.bfloat16),
+            (segment_ids // 128).astype(jnp.bfloat16),
+        ]
+    )
+    cuts = [tokens_dev * width, tokens_dev * (width + n_tm)]
+    cuts += [cuts[1] + rows, cuts[1] + 2 * rows]
+    depth, columns = qkv_weight.shape
+    small = jnp.pad(small, (0, -cuts[3] % columns)).reshape(-1, columns)
+    gathered = lax.all_gather(jnp.concatenate([qkv_weight, small], axis=0), "tm", axis=0)
+    weight = gathered[:, :depth].reshape(n_tm * depth, columns)
+    small_all = gathered[:, depth:].reshape(n_tm, -1)
+    all_queries = small_all[:, : cuts[0]].reshape(n_tm * tokens_dev, width)
+    all_masks = small_all[:, cuts[0] : cuts[1]].reshape(n_tm * tokens_dev, n_tm)
+    seg_low = small_all[:, cuts[1] : cuts[2]].reshape(-1).astype(jnp.int32)
+    seg_high = small_all[:, cuts[2] : cuts[3]].reshape(-1).astype(jnp.int32)
+    seg_all = jnp.pad(seg_high * 128 + seg_low, (4 * rows, 4 * rows))
+    seg_wide = lax.dynamic_slice_in_dim(seg_all, device * rows, 9 * rows, 0)
     values_in = stem.astype(jnp.float32)
     mean = jnp.mean(values_in, axis=-1, keepdims=True)
     var = jnp.mean((values_in - mean) ** 2, axis=-1, keepdims=True)
     normed = ((values_in - mean) * lax.rsqrt(var + 1e-05) * norm_gain).astype(jnp.bfloat16)
     projected = jnp.dot(
         normed,
-        lax.all_gather(qkv_weight, "tm", axis=0, tiled=True),
+        weight,
         preferred_element_type=jnp.float32,
     ).astype(jnp.bfloat16)
     query_part = projected[:, :width]
     keyvals = projected[:, width:]
     kv_pieces = []
-    seg_pieces = []
     for offset in range(-4, 5):
         if offset == 0:
             kv_pieces.append(keyvals)
-            seg_pieces.append(segment_ids)
         else:
             kv_pieces.append(from_behind(keyvals, "tm", -offset))
-            seg_pieces.append(from_behind(segment_ids, "tm", -offset))
     extended = jnp.concatenate(kv_pieces, axis=0)
-    seg_wide = jnp.concatenate(seg_pieces, axis=0)
     same = segment_ids[:, None] == seg_wide[None, :]
     group = math.gcd(heads, 4)
     span = group * HD
@@ -66,11 +86,7 @@
     contexts = lax.map(attend, jnp.arange(groups, dtype=jnp.int32))
     context = jnp.transpose(contexts, (1, 0, 2)).reshape(rows, width)
     memory = (values_in + context).astype(jnp.bfloat16)
-    tokens_dev = dec_queries.shape[0]
-    all_queries = lax.all_gather(dec_queries, "tm", axis=0, tiled=True)
-    all_masks = lax.all_gather(stretch_mask, "tm", axis=0, tiled=True)
     total_tokens = all_queries.shape[0]
-    device = lax.axis_index("tm")
     column = lax.dynamic_slice_in_dim(all_masks, device, 1, 1)[:, 0]
     owner = jnp.arange(total_tokens, dtype=jnp.int32) // tokens_dev
     allowed = (column == 1) | (owner == device)
@@ -92,11 +108,13 @@
         preferred_element_type=jnp.float32,
     )
     top_masked = jnp.transpose(jnp.where(allowed[None, :], local_top, jnp.float32(-1e30)))
-    num_all, top_all, den_all = (
-        lax.all_to_all(numer[None], "tm", split_axis=1, concat_axis=0, tiled=True),
-        lax.all_to_all(top_masked[None], "tm", split_axis=1, concat_axis=0, tiled=True),
-        lax.all_to_all(denom[None], "tm", split_axis=1, concat_axis=0, tiled=True),
-    )
+    packed = jnp.concatenate([numer.reshape(total_tokens, width), top_masked, denom], axis=1)
+    packed = jnp.pad(packed, ((0, 0), (0, -packed.shape[1] % 128)))
+    packed = packed.reshape(n_tm, tokens_dev, -1)
+    got = lax.all_to_all(packed, "tm", split_axis=0, concat_axis=0, tiled=True)
+    num_all = got[..., :width].reshape(n_tm, tokens_dev, heads, HD)
+    top_all = got[..., width : width + heads]
+    den_all = got[..., width + heads : width + 2 * heads]
     best = jnp.max(top_all, axis=0)
     factor = jnp.exp(top_all - best[None])
     num_total = jnp.sum(factor[..., None] * num_all, axis=0)

time: 602 us -> 450 us (0.75)
  blocking collectives: 230 us -> 0 us
  waiting for transfers between devices: 123 us -> 221 us
  starting transfers between devices: 131 us -> 113 us
    all_gather x2 -> x0, blocking collectives: 230 us -> none  [the longest x1 116 us: on_device(): all_masks = lax.all_gather(stretch_mask, 'tm', axis=0, tiled=True)]
    all_gather x1, waiting for transfers between devices: 0.02 us -> 134 us  [on_device(): lax.all_gather(jnp.concatenate([qkv_weight, small], axis=0), 'tm', axis=0)]
    ppermute x16 -> x8, starting transfers between devices: 83.2 us -> 52.3 us  [from_behind(): return lax.ppermute(block, axis, route)]
    ppermute x16 -> x8, waiting for transfers between devices: 74.5 us -> 49.9 us  [from_behind(): return lax.ppermute(block, axis, route)]
    reshape x1 -> x7, local copies, waits for them, and re-layouts: 0.6 us -> 16.1 us  [the longest x1 13.7 us: on_device(): weight = gathered[:, :depth].reshape(n_tm * depth, columns)]
    unnamed x30 -> x18, local copies, waits for them, and re-layouts: 35.9 us -> 22.6 us
    all_to_all x3 -> x1, starting transfers between devices: 48 us -> 60.5 us  [on_device(): got = lax.all_to_all(packed, 'tm', split_axis=0, concat_axis=0, tiled=True)]
    all_to_all x3 -> x1, waiting for transfers between devices: 47.8 us -> 36.4 us  [on_device(): got = lax.all_to_all(packed, 'tm', split_axis=0, concat_axis=0, tiled=True)]
  transfers between devices with their start and end apart: 20 -> 10, of which waited for: 9 -> 5; matrix products, arithmetic and copies ran while one was open for 7% -> 4% of each run, Pallas kernels for 0% -> 0%
where the time goes in v1:
time: 450 us; the launch traced here: 448 us
  waiting for transfers between devices  221 us (49%)
  starting transfers between devices  113 us (25%)
  local copies, waits for them, and re-layouts  60.3 us (13%)
  matrix products  29.6 us (7%)
  between operations  14.2 us (3%)
  other arithmetic  7.12 us (2%)
    all_gather x1, waiting for transfers between devices, on_device(): lax.all_gather(jnp.concatenate([qkv_weight, small], axis=0), 'tm', axis=0)  134 us
    all_to_all x1, starting transfers between devices, on_device(): got = lax.all_to_all(packed, 'tm', split_axis=0, concat_axis=0, tiled=True)  60.5 us
    ppermute x8, starting transfers between devices, from_behind(): return lax.ppermute(block, axis, route)  52.3 us
    ppermute x8, waiting for transfers between devices, from_behind(): return lax.ppermute(block, axis, route)  49.9 us
    all_to_all x1, waiting for transfers between devices, on_device(): got = lax.all_to_all(packed, 'tm', split_axis=0, concat_axis=0, tiled=True)  36.4 us
    unnamed x18, local copies, waits for them, and re-layouts  22.6 us
    reshape x1, local copies, waits for them, and re-layouts, on_device(): weight = gathered[:, :depth].reshape(n_tm * depth, columns)  13.7 us
    sub x5, matrix products, attend(): raised = jnp.exp(scores - top)  11.9 us
  transfers between devices with their start and end apart: 10, of which 5 were waited for; matrix products, arithmetic and copies ran while one was open for 4% of the time, Pallas kernels for 0%

profile of v1, /device:TPU:1, one launch (start us, length us, event | category | flops | bytes accessed | tf_op | source)
XLA Modules:
  0.0 448.3 jit_solution(17356264649642156661)
XLA Ops:
  7.2 0.7 convert_element_type.47
  8.0 0.7 fusion.37
  8.6 0.7 reshape.134
  9.4 1.6 maximum_bitcast_fusion
  11.0 1.2 copy.34
  12.6 134.4 %all-gather.4.cloned.1.call-done = bf16[64,21,3840]{2,1,0:T(8,128)(2,1)} async-done(((bf16[1,21,3840]{2,1,0:T(8,128)(2,1)}), bf16[64,21,3840]{2,1,0:T(8,128)(2,1)}) %all-gather.4.cloned.1.call-update) | async-done | bytes 10321936 | tf_op jit(solution)/shard_map/all_gather | solution.py:36
  147.0 13.7 %reshape.137 = bf16[1280,3840]{1,0:T(8,128)(2,1)} reshape(bf16[64,20,3840]{2,1,0:T(8,128)(2,1)} %bitcast.52) | data formatting | bytes 19660800 | tf_op jit(solution)/shard_map/reshape | solution.py:37
  160.7 5.3 %convolution_convert_fusion = bf16[128,3840]{1,0:T(8,128)(2,1)S(1)} fusion(bf16[1280,3840]{1,0:T(8,128)(2,1)} %reshape.137, bf16[128,1280]{0,1:T(8,128)(2,1)S(1)} %copy.34, f32[1280]{0:T(1024)S(1)} %copy-done.2, f32[128]{0:T(128)S(1)} %add_rsqrt_fusion, f32[128]{0:T(128)S(1)} %broadcast_multiply_fusion), kind=kOutput, calls=%fused_computation.16 | convolution fusion | flops 1259601920 | bytes 11147264 | tf_op jit(solution)/shard_map/dot_general | solution.py:49
  166.0 1.0 slice.45
  167.0 4.0 collective-permute-start
  171.0 3.1 slice.47
  174.2 1.3 collective-permute-start.7
  175.5 1.3 collective-permute-start.6
  176.8 1.3 collective-permute-start.5
  178.1 7.7 %collective-permute-start.1 = (bf16[128,2560]{1,0:T(8,128)(2,1)}, bf16[128,2560]{1,0:T(8,128)(2,1)}, u32[]{:S(2)}, u32[]{:S(2)}) collective-permute-start(bf16[128,2560]{1,0:T(8,128)(2,1)} %slice.45), channel_id=1, source_target_pairs={{0,3},{1,4},{2,5},{3,6},{4,7},{5,8},{6,9},{7,10},{8,11},{9,12},{10... | collective-permute-start | bytes 1966088 | tf_op jit(solution)/shard_map/ppermute | solution.py:14
  186.0 0.6 reshape_reshape.3
  186.9 22.3 %collective-permute-start.2 = (bf16[128,2560]{1,0:T(8,128)(2,1)}, bf16[128,2560]{1,0:T(8,128)(2,1)S(1)}, u32[]{:S(2)}, u32[]{:S(2)}) collective-permute-start(bf16[128,2560]{1,0:T(8,128)(2,1)} %slice.45), channel_id=1, source_target_pairs={{0,2},{1,3},{2,4},{3,5},{4,6},{5,7},{6,8},{7,9},{8,10},{9,11},{10,... | collective-permute-start | bytes 1966088 | tf_op jit(solution)/shard_map/ppermute | solution.py:14
  209.2 2.0 constant_dynamic-update-slice_fusion.9
  211.2 12.4 %collective-permute-start.3 = (bf16[128,2560]{1,0:T(8,128)(2,1)}, bf16[128,2560]{1,0:T(8,128)(2,1)S(1)}, u32[]{:S(2)}, u32[]{:S(2)}) collective-permute-start(bf16[128,2560]{1,0:T(8,128)(2,1)} %slice.45), channel_id=1, source_target_pairs={{0,1},{1,2},{2,3},{3,4},{4,5},{5,6},{6,7},{7,8},{8,9},{9,10},{10,1... | collective-permute-start | bytes 1966088 | tf_op jit(solution)/shard_map/ppermute | solution.py:14
  223.6 2.0 constant_dynamic-update-slice_fusion.8
  225.6 1.9 collective-permute-start.4
  227.5 0.9 constant_dynamic-update-slice_fusion.7
  228.4 3.1 collective-permute-done.3
  231.4 0.9 constant_dynamic-update-slice_fusion.6
  232.4 0.9 constant_dynamic-update-slice_fusion.5
  233.3 35.1 %collective-permute-done.4 = bf16[128,2560]{1,0:T(8,128)(2,1)S(1)} collective-permute-done((bf16[128,2560]{1,0:T(8,128)(2,1)}, bf16[128,2560]{1,0:T(8,128)(2,1)S(1)}, u32[]{:S(2)}, u32[]{:S(2)}) %collective-permute-start.4) | collective-permute-done | bytes 655392 | tf_op jit(solution)/shard_map/ppermute | solution.py:14
  268.4 0.9 constant_dynamic-update-slice_fusion.4
  269.3 2.0 constant_dynamic-update-slice_fusion.3
  271.3 11.8 %collective-permute-done.6 = bf16[128,2560]{1,0:T(8,128)(2,1)} collective-permute-done((bf16[128,2560]{1,0:T(8,128)(2,1)}, bf16[128,2560]{1,0:T(8,128)(2,1)}, u32[]{:S(2)}, u32[]{:S(2)}) %collective-permute-start.6) | collective-permute-done | bytes 655392 | tf_op jit(solution)/shard_map/ppermute | solution.py:14
  283.0 2.0 constant_dynamic-update-slice_fusion.2
  285.0 2.0 constant_dynamic-update-slice_fusion.1
  287.0 8.9 %copy.36 = bf16[1152,2560]{0,1:T(8,128)(2,1)} copy(bf16[1152,2560]{1,0:T(8,128)(2,1)} %constant_dynamic-update-slice_fusion.1) | data formatting | bytes 11796480
  295.9 41.2 %while.13 = (s32[]{:T(128)}, f32[5,128,256]{1,2,0:T(8,128)}, s32[5]{0:T(128)S(1)}, bf16[1152,2560]{0,1:T(8,128)(2,1)}, bf16[128,1280]{1,0:T(8,128)(2,1)S(1)}, /*...) while((s32[]{:T(128)}, f32[5,128,256]{1,2,0:T(8,128)}, ...), condition=%wide.region_5.6_spmd.clone, body=%wide.region_2.5_spmd.clone.sunk | while | flops 154682496 | bytes 9282826 | solution.py:86
  295.9 0.6 dynamic_slice.47
  297.4 1.3 constant_dynamic-slice_fusion.5
  298.8 2.4 fusion.56
  301.2 2.3 fusion.57
  303.5 0.7 constant_dynamic-update-slice_fusion.11
  304.1 0.6 dynamic_slice.47
  305.7 1.3 constant_dynamic-slice_fusion.5
  307.0 2.4 fusion.56
  309.4 2.3 fusion.57
  311.7 0.7 constant_dynamic-update-slice_fusion.11
  312.4 0.6 dynamic_slice.47
  313.9 1.3 constant_dynamic-slice_fusion.5
  315.3 2.4 fusion.56
  317.6 2.3 fusion.57
  320.0 0.7 constant_dynamic-update-slice_fusion.11
  320.6 0.6 dynamic_slice.47
  322.2 1.3 constant_dynamic-slice_fusion.5
  323.5 2.4 fusion.56
  325.9 2.3 fusion.57
  328.2 0.7 constant_dynamic-update-slice_fusion.11
  330.4 1.3 constant_dynamic-slice_fusion.5
  331.8 2.4 fusion.56
  334.1 2.3 fusion.57
  336.4 0.7 constant_dynamic-update-slice_fusion.11
  337.1 1.2 fusion.17
  338.3 0.6 fusion.41
  340.0 1.3 reshape.143
  341.3 60.5 %all-to-all-start = ((f32[64,2,1408]{2,1,0:T(2,128)}), f32[64,2,1408]{2,1,0:T(2,128)S(1)}, u32[]{:S(2)}, u32[]{:S(2)}) async-start(f32[64,2,1408]{2,1,0:T(2,128)} %reshape.143), calls=%async_computation | async-start | bytes 1441792 | tf_op jit(solution)/shard_map/all_to_all | solution.py:114
  401.9 0.9 copy.45
  402.8 36.4 %all-to-all-done = f32[64,2,1408]{2,1,0:T(2,128)S(1)} async-done(((f32[64,2,1408]{2,1,0:T(2,128)}), f32[64,2,1408]{2,1,0:T(2,128)S(1)}, u32[]{:S(2)}, u32[]{:S(2)}) %all-to-all-start) | async-done | bytes 720928 | tf_op jit(solution)/shard_map/all_to_all | solution.py:114
  440.9 0.6 divide_convert_fusion.2
  (64 shorter events, 5.9 us)
Async XLA Ops:
  7.2 139.8 %all-gather.4.cloned.1.call-start = ((), (), s32[]{:S(2)}) async-start(), calls=%async_computation.1 | async-start | bytes 11980800 | tf_op jit(solution)/shard_map/all_gather | solution.py:36
  147.0 13.7 %copy-start.2 = (f32[1280]{0:T(1024)S(1)}, f32[1280]{0:T(1024)}, u32[]{:S(2)}) copy-start(f32[1280]{0:T(1024)} %param.9) | copy-start | bytes 15364
  166.0 66.3 %copy-start = (bf16[128,3840]{1,0:T(8,128)(2,1)}, bf16[128,3840]{1,0:T(8,128)(2,1)S(1)}, u32[]{:S(2)}) copy-start(bf16[128,3840]{1,0:T(8,128)(2,1)S(1)} %convolution_convert_fusion) | copy-start | bytes 2949124
  167.0 19.9 %collective-permute-start = (bf16[128,2560]{1,0:T(8,128)(2,1)}, bf16[128,2560]{1,0:T(8,128)(2,1)}, u32[]{:S(2)}, u32[]{:S(2)}) collective-permute-start(bf16[128,2560]{1,0:T(8,128)(2,1)} %slice.45), channel_id=1, source_target_pairs={{0,4},{1,5},{2,6},{3,7},{4,8},{5,9},{6,10},{7,11},{8,12},{9,13},{1... | collective-permute-start | bytes 1966088 | tf_op jit(solution)/shard_map/ppermute | solution.py:14
  174.2 110.8 %collective-permute-start.7 = (bf16[128,2560]{1,0:T(8,128)(2,1)}, bf16[128,2560]{1,0:T(8,128)(2,1)}, u32[]{:S(2)}, u32[]{:S(2)}) collective-permute-start(bf16[128,2560]{1,0:T(8,128)(2,1)} %slice.45), channel_id=1, source_target_pairs={{4,0},{5,1},{6,2},{7,3},{8,4},{9,5},{10,6},{11,7},{12,8},{13,9},{1... | collective-permute-start | bytes 1966088 | tf_op jit(solution)/shard_map/ppermute | solution.py:14
  175.5 107.5 %collective-permute-start.6 = (bf16[128,2560]{1,0:T(8,128)(2,1)}, bf16[128,2560]{1,0:T(8,128)(2,1)}, u32[]{:S(2)}, u32[]{:S(2)}) collective-permute-start(bf16[128,2560]{1,0:T(8,128)(2,1)} %slice.45), channel_id=1, source_target_pairs={{3,0},{4,1},{5,2},{6,3},{7,4},{8,5},{9,6},{10,7},{11,8},{12,9},{13... | collective-permute-start | bytes 1966088 | tf_op jit(solution)/shard_map/ppermute | solution.py:14
  176.8 92.4 %collective-permute-start.5 = (bf16[128,2560]{1,0:T(8,128)(2,1)}, bf16[128,2560]{1,0:T(8,128)(2,1)}, u32[]{:S(2)}, u32[]{:S(2)}) collective-permute-start(bf16[128,2560]{1,0:T(8,128)(2,1)} %slice.45), channel_id=1, source_target_pairs={{2,0},{3,1},{4,2},{5,3},{6,4},{7,5},{8,6},{9,7},{10,8},{11,9},{12,... | collective-permute-start | bytes 1966088 | tf_op jit(solution)/shard_map/ppermute | solution.py:14
  178.1 33.0 %collective-permute-start.1 = (bf16[128,2560]{1,0:T(8,128)(2,1)}, bf16[128,2560]{1,0:T(8,128)(2,1)}, u32[]{:S(2)}, u32[]{:S(2)}) collective-permute-start(bf16[128,2560]{1,0:T(8,128)(2,1)} %slice.45), channel_id=1, source_target_pairs={{0,3},{1,4},{2,5},{3,6},{4,7},{5,8},{6,9},{7,10},{8,11},{9,12},{10... | collective-permute-start | bytes 1966088 | tf_op jit(solution)/shard_map/ppermute | solution.py:14
  186.9 38.7 %collective-permute-start.2 = (bf16[128,2560]{1,0:T(8,128)(2,1)}, bf16[128,2560]{1,0:T(8,128)(2,1)S(1)}, u32[]{:S(2)}, u32[]{:S(2)}) collective-permute-start(bf16[128,2560]{1,0:T(8,128)(2,1)} %slice.45), channel_id=1, source_target_pairs={{0,2},{1,3},{2,4},{3,5},{4,6},{5,7},{6,8},{7,9},{8,10},{9,11},{10,... | collective-permute-start | bytes 1966088 | tf_op jit(solution)/shard_map/ppermute | solution.py:14
  211.2 20.3 %collective-permute-start.3 = (bf16[128,2560]{1,0:T(8,128)(2,1)}, bf16[128,2560]{1,0:T(8,128)(2,1)S(1)}, u32[]{:S(2)}, u32[]{:S(2)}) collective-permute-start(bf16[128,2560]{1,0:T(8,128)(2,1)} %slice.45), channel_id=1, source_target_pairs={{0,1},{1,2},{2,3},{3,4},{4,5},{5,6},{6,7},{7,8},{8,9},{9,10},{10,1... | collective-permute-start | bytes 1966088 | tf_op jit(solution)/shard_map/ppermute | solution.py:14
  225.6 42.8 %collective-permute-start.4 = (bf16[128,2560]{1,0:T(8,128)(2,1)}, bf16[128,2560]{1,0:T(8,128)(2,1)S(1)}, u32[]{:S(2)}, u32[]{:S(2)}) collective-permute-start(bf16[128,2560]{1,0:T(8,128)(2,1)} %slice.45), channel_id=1, source_target_pairs={{1,0},{2,1},{3,2},{4,3},{5,4},{6,5},{7,6},{8,7},{9,8},{10,9},{11,1... | collective-permute-start | bytes 1966088 | tf_op jit(solution)/shard_map/ppermute | solution.py:14
  287.0 8.9 %slice-start = ((bf16[128,3840]{1,0:T(8,128)(2,1)}), bf16[128,1280]{1,0:T(8,128)(2,1)S(1)}, s32[]{:S(2)}) async-start(bf16[128,3840]{1,0:T(8,128)(2,1)} %copy-done), calls=%async_computation.2 | async-start | bytes 655360 | tf_op jit(solution)/shard_map/slice | solution.py:54
  287.0 8.9 %copy-start.1 = (s32[128]{0:T(128)S(1)}, s32[128]{0:T(128)}, u32[]{:S(2)}) copy-start(s32[128]{0:T(128)} %param.11) | copy-start | bytes 1540
  341.3 97.8 %all-to-all-start = ((f32[64,2,1408]{2,1,0:T(2,128)}), f32[64,2,1408]{2,1,0:T(2,128)S(1)}, u32[]{:S(2)}, u32[]{:S(2)}) async-start(f32[64,2,1408]{2,1,0:T(2,128)} %reshape.143), calls=%async_computation | async-start | bytes 1441792 | tf_op jit(solution)/shard_map/all_to_all | solution.py:114
Sparse Core Ops, SparseCore 0:
  11.2 135.7 all-gather.3

commit v2 on v1

v2 whole, which is shorter than its diff:
```python
import functools
import math

import jax
import jax.numpy as jnp
from jax import lax
from jax.experimental import pallas as pl
from jax.experimental.pallas import tpu as pltpu
from jax.sharding import PartitionSpec as P

HD = 64
NZ = 8
REACH = 2
MESH = pl.DeviceIdType.MESH


def gather_kernel(nx, w_ref, stem_ref, wide_ref, halo_ref, w_recv, w_zs, w_xs, w_ps, h_recv, h_zs, h_ps, own_sem):
    me = lax.axis_index("tm")
    core = lax.rem(me, 2)
    chip = me // 2
    z = lax.rem(chip, NZ)
    x = chip // NZ
    chips = nx * NZ

    def index(xx, zz):
        return (xx * NZ + zz) * 2 + core

    right_x, left_x, far_x = lax.rem(x + 1, nx), lax.rem(x + nx - 1, nx), lax.rem(x + 2, nx)
    right, left = index(right_x, z), index(left_x, z)
    partner = me + 1 - 2 * core
    up, down = me + 2, me - 2
    has_up, has_down = z < NZ - 1, z > 0
    has_next, has_prev = chip < chips - 1, chip > 0

    barrier = pltpu.get_barrier_semaphore()

    def greet(peer):
        pl.semaphore_signal(barrier, inc=1, device_id={"tm": peer}, device_id_type=MESH)

    greet(right)
    greet(left)
    greet(partner)

    @pl.when(has_next)
    def _():
        greet(up)

    @pl.when(has_prev)
    def _():
        greet(down)

    pl.semaphore_wait(barrier, 3 + has_next.astype(jnp.int32) + has_prev.astype(jnp.int32))

    def w_copy(shard, peer, send_sem, own=False):
        return pltpu.make_async_remote_copy(
            src_ref=w_ref if own else wide_ref.at[shard],
            dst_ref=wide_ref.at[shard],
            send_sem=send_sem,
            recv_sem=w_recv.at[shard],
            device_id={"tm": peer},
            device_id_type=MESH,
        )

    def h_copy(from_slot, to_slot, peer, send_sem, own=False):
        return pltpu.make_async_remote_copy(
            src_ref=stem_ref if own else halo_ref.at[from_slot],
            dst_ref=halo_ref.at[to_slot],
            send_sem=send_sem,
            recv_sem=h_recv.at[to_slot],
            device_id={"tm": peer},
            device_id_type=MESH,
        )

    def to_right(xx, zz, slot, own=False):
        return w_copy(index(xx, zz), right, w_xs.at[0, slot * NZ + zz], own)

    def to_left(xx, zz, slot, own=False):
        return w_copy(index(xx, zz), left, w_xs.at[1, slot * NZ + zz], own)

    def to_partner(xx, zz, own=False):
        return w_copy(index(xx, zz), partner, w_ps.at[xx * NZ + zz], own)

    def to_up(zz, own=False):
        return w_copy(index(x, zz), up, w_zs.at[0, zz], own)

    def to_down(zz, own=False):
        return w_copy(index(x, zz), down, w_zs.at[1, zz], own)

    def slot_of(step, cc):
        return (step + REACH) * 2 + cc

    own_slot = slot_of(0, core)
    h_next = h_copy(own_slot, slot_of(-1, core), up, h_zs.at[0], True)
    h_prev = h_copy(own_slot, slot_of(1, core), down, h_zs.at[1], True)
    h_own = h_copy(own_slot, own_slot, partner, h_ps.at[2], True)
    relay_next = h_copy(slot_of(-1, core), slot_of(-2, core), up, h_zs.at[2])
    relay_prev = h_copy(slot_of(1, core), slot_of(2, core), down, h_zs.at[3])

    def h_pass(step):
        slot = slot_of(step, core)
        return h_copy(slot, slot, partner, h_ps.at[step + REACH])

    def w_arrived(shard):
        pltpu.make_async_copy(wide_ref.at[shard], wide_ref.at[shard], w_recv.at[shard]).wait()

    def h_arrived(slot):
        pltpu.make_async_copy(halo_ref.at[slot], halo_ref.at[slot], h_recv.at[slot]).wait()

    @pl.when(has_up)
    def _():
        to_up(z, True).start()

    @pl.when(has_down)
    def _():
        to_down(z, True).start()

    @pl.when(has_next)
    def _():
        h_next.start()

    @pl.when(has_prev)
    def _():
        h_prev.start()

    to_right(x, z, 0, True).start()
    to_left(x, z, 0, True).start()
    to_partner(x, z, True).start()
    h_own.start()
    own_w = pltpu.make_async_copy(w_ref, wide_ref.at[me], own_sem.at[0])
    own_h = pltpu.make_async_copy(stem_ref, halo_ref.at[own_slot], own_sem.at[1])
    own_w.start()
    own_h.start()

    def beside(zz, fresh):
        ok = (zz >= 0) & (zz < NZ) & fresh

        @pl.when(ok)
        def _():
            even = lax.rem(zz, 2) == 0
            w_arrived(index(left_x, zz))
            to_partner(left_x, zz).start()

            @pl.when(even)
            def _():
                to_right(left_x, zz, 1).start()

            w_arrived(index(right_x, zz))
            to_partner(right_x, zz).start()

            @pl.when(jnp.logical_not(even))
            def _():
                to_left(right_x, zz, 1).start()

    def far(zz, fresh):
        @pl.when((zz >= 0) & (zz < NZ) & fresh)
        def _():
            w_arrived(index(far_x, zz))
            to_partner(far_x, zz).start()

    def step(s, carry):
        below, above = z - s, z + s

        @pl.when((below >= 0) & (s > 0) & (s < NZ))
        def _():
            w_arrived(index(x, below))

            @pl.when(has_up)
            def _():
                to_up(below).start()

            to_right(x, below, 0).start()
            to_left(x, below, 0).start()
            to_partner(x, below).start()

        @pl.when((above < NZ) & (s > 0))
        def _():
            w_arrived(index(x, above))

            @pl.when(has_down)
            def _():
                to_down(above).start()

            to_right(x, above, 0).start()
            to_left(x, above, 0).start()
            to_partner(x, above).start()

        beside(z - (s - 1), s >= 1)
        beside(z + (s - 1), s >= 2)
        far(z - (s - 2), s >= 2)
        far(z + (s - 2), s >= 3)
        return carry

    lax.fori_loop(1, 4, step, 0)

    @pl.when(has_prev)
    def _():
        h_arrived(slot_of(-1, core))
        h_pass(-1).start()

        @pl.when(has_next)
        def _():
            relay_next.start()

    @pl.when(has_next)
    def _():
        h_arrived(slot_of(1, core))
        h_pass(1).start()

        @pl.when(has_prev)
        def _():
            relay_prev.start()

    lax.fori_loop(4, NZ + 2, step, 0)

    @pl.when(chip >= 2)
    def _():
        h_arrived(slot_of(-2, core))
        h_pass(-2).start()

    @pl.when(chip < chips - 2)
    def _():
        h_arrived(slot_of(2, core))
        h_pass(2).start()

    def settle(i, carry):
        w_arrived(i * 2 + 1 - core)
        to_partner(i // NZ, lax.rem(i, NZ), False).wait_send()
        return carry

    lax.fori_loop(0, chips, settle, 0)

    def settle_z(zz, carry):
        @pl.when((zz <= z) & has_up)
        def _():
            to_up(zz).wait_send()

        @pl.when((zz >= z) & has_down)
        def _():
            to_down(zz).wait_send()

        to_right(x, zz, 0).wait_send()
        to_left(x, zz, 0).wait_send()
        even = lax.rem(zz, 2) == 0

        @pl.when(even)
        def _():
            to_right(left_x, zz, 1).wait_send()

        @pl.when(jnp.logical_not(even))
        def _():
            to_left(right_x, zz, 1).wait_send()

        return carry

    lax.fori_loop(0, NZ, settle_z, 0)

    def other(step):
        h_arrived(slot_of(step, 1 - core))

    other(0)
    h_own.wait_send()

    @pl.when(has_next)
    def _():
        h_next.wait_send()
        h_pass(1).wait_send()
        other(1)

    @pl.when(has_prev)
    def _():
        h_prev.wait_send()
        h_pass(-1).wait_send()
        other(-1)

    @pl.when(has_next & has_prev)
    def _():
        relay_next.wait_send()
        relay_prev.wait_send()

    @pl.when(chip >= 2)
    def _():
        h_pass(-2).wait_send()
        other(-2)

    @pl.when(chip < chips - 2)
    def _():
        h_pass(2).wait_send()
        other(2)

    own_w.wait()
    own_h.wait()


def gather(wide, stem, n_tm):
    nx = n_tm // (2 * NZ)
    dma = pltpu.SemaphoreType.DMA
    return pl.pallas_call(
        functools.partial(gather_kernel, nx),
        out_shape=(
            jax.ShapeDtypeStruct((n_tm, *wide.shape), wide.dtype),
            jax.ShapeDtypeStruct((4 * REACH + 2, *stem.shape), stem.dtype),
        ),
        in_specs=[pl.BlockSpec(memory_space=pltpu.VMEM)] * 2,
        out_specs=(pl.BlockSpec(memory_space=pl.ANY), pl.BlockSpec(memory_space=pl.ANY)),
        scratch_shapes=[
            dma((n_tm,)),
            dma((2, NZ)),
            dma((2, 2 * NZ)),
            dma((n_tm // 2,)),
            dma((4 * REACH + 2,)),
            dma((4,)),
            dma((2 * REACH + 1,)),
            dma((2,)),
        ],
        compiler_params=pltpu.CompilerParams(collective_id=0, has_side_effects=True),
        name="gather",
    )(wide, stem)


def deal_kernel(n, out_ref, in_ref, send_sem, recv_sem, own_sem):
    me = lax.axis_index("tm")
    barrier = pltpu.get_barrier_semaphore()

    def peer_of(i):
        return lax.rem(me + i, n)

    def greet(i, carry):
        pl.semaphore_signal(barrier, inc=1, device_id={"tm": peer_of(i)}, device_id_type=MESH)
        return carry

    lax.fori_loop(1, n, greet, 0)
    own = pltpu.make_async_copy(out_ref.at[me], in_ref.at[me], own_sem)
    own.start()
    pl.semaphore_wait(barrier, n - 1)

    def copy(i):
        peer = peer_of(i)
        return pltpu.make_async_remote_copy(
            src_ref=out_ref.at[peer],
            dst_ref=in_ref.at[me],
            send_sem=send_sem.at[i],
            recv_sem=recv_sem.at[me],
            device_id={"tm": peer},
            device_id_type=MESH,
        )

    def send(i, carry):
        copy(i).start()
        return carry

    lax.fori_loop(1, n, send, 0)
    own.wait()

    def settle(i, carry):
        peer = peer_of(i)
        pltpu.make_async_copy(in_ref.at[peer], in_ref.at[peer], recv_sem.at[peer]).wait()
        copy(i).wait_send()
        return carry

    lax.fori_loop(1, n, settle, 0)


def deal(payload):
    n = payload.shape[0]
    dma = pltpu.SemaphoreType.DMA
    return pl.pallas_call(
        functools.partial(deal_kernel, n),
        out_shape=jax.ShapeDtypeStruct(payload.shape, payload.dtype),
        in_specs=[pl.BlockSpec(memory_space=pltpu.VMEM)],
        out_specs=pl.BlockSpec(memory_space=pltpu.VMEM),
        scratch_shapes=[dma((n,)), dma((n,)), dma],
        compiler_params=pltpu.CompilerParams(collective_id=1, has_side_effects=True),
        name="deal",
    )(payload)


def layer_norm(block, gain):
    values_in = block.astype(jnp.float32)
    mean = jnp.mean(values_in, axis=-1, keepdims=True)
    var = jnp.mean((values_in - mean) ** 2, axis=-1, keepdims=True)
    return ((values_in - mean) * lax.rsqrt(var + 1e-05) * gain).astype(jnp.bfloat16)


def two_parts(value):
    high = lax.reduce_precision(value, 8, 7)
    return high, lax.reduce_precision(value - high, 8, 7)


def on_device(stem, norm_gain, qkv_weight, segment_ids, dec_queries, stretch_mask):
    rows, width = stem.shape
    heads = width // HD
    scale = HD ** (-0.5)
    tokens_dev = dec_queries.shape[0]
    n_tm = lax.axis_size("tm")
    device = lax.axis_index("tm")
    small = jnp.concatenate(
        [
            dec_queries.reshape(-1),
            stretch_mask.astype(jnp.bfloat16).reshape(-1),
            (segment_ids % 128).astype(jnp.bfloat16),
            (segment_ids // 128).astype(jnp.bfloat16),
        ]
    )
    cuts = [tokens_dev * width, tokens_dev * (width + n_tm)]
    cuts += [cuts[1] + rows, cuts[1] + 2 * rows]
    depth, columns = qkv_weight.shape
    small = jnp.pad(small, (0, -cuts[3] % columns)).reshape(-1, columns)
    gathered, halo = gather(jnp.concatenate([qkv_weight, small], axis=0), stem, n_tm)
    weight = gathered[:, :depth].reshape(n_tm * depth, columns)
    small_all = gathered[:, depth:].reshape(n_tm, -1)
    all_queries = small_all[:, : cuts[0]].reshape(n_tm * tokens_dev, width)
    all_masks = small_all[:, cuts[0] : cuts[1]].reshape(n_tm * tokens_dev, n_tm)
    seg_low = small_all[:, cuts[1] : cuts[2]].reshape(-1).astype(jnp.int32)
    seg_high = small_all[:, cuts[2] : cuts[3]].reshape(-1).astype(jnp.int32)
    around = halo.shape[0]
    seg_all = jnp.pad(seg_high * 128 + seg_low, (2 * REACH * rows, 2 * REACH * rows))
    chip = device // 2
    seg_wide = lax.dynamic_slice_in_dim(seg_all, chip * 2 * rows, around * rows, 0)
    block_at = chip * 2 - 2 * REACH + jnp.arange(around, dtype=jnp.int32)
    exists = (block_at >= 0) & (block_at < n_tm)
    halo = jnp.where(exists[:, None, None], halo, jnp.bfloat16(0)).reshape(around * rows, width)
    query_part = jnp.dot(
        layer_norm(stem, norm_gain), weight[:, :width], preferred_element_type=jnp.float32
    ).astype(jnp.bfloat16)
    extended = jnp.dot(
        layer_norm(halo, norm_gain), weight[:, width:], preferred_element_type=jnp.float32
    ).astype(jnp.bfloat16)
    same = segment_ids[:, None] == seg_wide[None, :]
    group = math.gcd(heads, 4)
    span = group * HD
    groups = heads // group

    def attend(index):
        start = index * span
        query_group = lax.dynamic_slice_in_dim(query_part, start, span, 1).reshape(rows, group, HD)
        key_group = lax.dynamic_slice_in_dim(extended, start, span, 1).reshape(-1, group, HD)
        value_group = lax.dynamic_slice_in_dim(extended, width + start, span, 1).reshape(
            -1, group, HD
        )
        scores = (
            jnp.einsum("qhd,khd->hqk", query_group, key_group, preferred_element_type=jnp.float32)
            * scale
        )
        scores = jnp.where(same[None], scores, jnp.float32(-1e30))
        top = jnp.max(scores, axis=-1, keepdims=True)
        raised = jnp.exp(scores - top)
        probs = (raised / jnp.sum(raised, axis=-1, keepdims=True)).astype(jnp.bfloat16)
        context = jnp.einsum("hqk,khd->qhd", probs, value_group, preferred_element_type=jnp.float32)
        return context.reshape(rows, span)

    contexts = lax.map(attend, jnp.arange(groups, dtype=jnp.int32))
    context = jnp.transpose(contexts, (1, 0, 2)).reshape(rows, width)
    memory = (stem.astype(jnp.float32) + context).astype(jnp.bfloat16)
    total_tokens = all_queries.shape[0]
    column = lax.dynamic_slice_in_dim(all_masks, device, 1, 1)[:, 0]
    owner = jnp.arange(total_tokens, dtype=jnp.int32) // tokens_dev
    allowed = (column == 1) | (owner == device)
    query_heads = all_queries.reshape(total_tokens, heads, HD)
    memory_heads = memory.reshape(rows, heads, HD)
    cross = (
        jnp.einsum("thd,phd->htp", query_heads, memory_heads, preferred_element_type=jnp.float32)
        * scale
    )
    top_high, top_low = two_parts(jnp.max(cross, axis=-1))
    shift = top_high + top_low
    weights = jnp.where(
        allowed[None, :, None], jnp.exp(cross - shift[:, :, None]), jnp.float32(0.0)
    )
    den_high, den_low = two_parts(jnp.sum(weights, axis=-1))
    numer = jnp.einsum(
        "htp,phd->thd",
        weights.astype(jnp.bfloat16),
        memory_heads,
        preferred_element_type=jnp.float32,
    ).astype(jnp.bfloat16)
    top_high = jnp.where(allowed[None, :], top_high, jnp.float32(-1e30))
    top_low = jnp.where(allowed[None, :], top_low, jnp.float32(0.0))
    stats = jnp.stack([top_high, top_low, den_high, den_low]).astype(jnp.bfloat16)
    stats = jnp.transpose(stats, (2, 0, 1)).reshape(n_tm, -1)
    payload = jnp.concatenate([numer.reshape(n_tm, -1), stats], axis=1)
    payload = jnp.pad(payload, ((0, 0), (0, -payload.shape[1] % 2048)))
    got = deal(payload.reshape(n_tm, -1, 128)).reshape(n_tm, -1).astype(jnp.float32)
    num_all = got[:, : tokens_dev * width].reshape(n_tm, tokens_dev, heads, HD)
    stats = got[:, tokens_dev * width : tokens_dev * (width + 4 * heads)]
    stats = stats.reshape(n_tm, tokens_dev, 4, heads)
    top_all = stats[:, :, 0] + stats[:, :, 1]
    den_all = stats[:, :, 2] + stats[:, :, 3]
    best = jnp.max(top_all, axis=0)
    factor = jnp.exp(top_all - best[None])
    num_total = jnp.sum(factor[..., None] * num_all, axis=0)
    den_total = jnp.sum(factor * den_all, axis=0)
    cross_out = (num_total / den_total[..., None]).reshape(tokens_dev, width).astype(jnp.bfloat16)
    return (memory, cross_out)


def solution(mesh):
    placed = (
        P(("utt", "tm"), None),
        P(),
        P("tm", None),
        P(("utt", "tm")),
        P(("utt", "tm"), None),
        P(("utt", "tm"), None),
    )
    return jax.shard_map(
        on_device,
        mesh=mesh,
        in_specs=placed,
        out_specs=(P(("utt", "tm"), None), P(("utt", "tm"), None)),
        check_vma=False,
    )
```

time: 450 us -> 237 us (0.53)
  waiting for transfers between devices: 221 us -> 0 us
  Pallas kernels: 0 us -> 127 us
  starting transfers between devices: 113 us -> 0 us
  between operations: 14.2 us -> 0.95 us
  matrix products: 29.6 us -> 42.3 us
  local copies, waits for them, and re-layouts: 60.3 us -> 49.6 us
  other arithmetic: 7.12 us -> 12.5 us
    all_gather x1 -> x0, waiting for transfers between devices: 134 us -> none  [on_device(): lax.all_gather(jnp.concatenate([qkv_weight, small], axis=0), 'tm', axis=0)]
    pallas_call x0 -> x2, Pallas kernels: none -> 127 us  [the longest x1 88 us: gather(): pl.pallas_call(functools.partial(gather_kernel, nx), out_shape=(jax.Shape...]
    all_to_all x1 -> x0, starting transfers between devices: 60.5 us -> none  [on_device(): got = lax.all_to_all(packed, 'tm', split_axis=0, concat_axis=0, tiled=True)]
    ppermute x8 -> x0, starting transfers between devices: 52.3 us -> none  [from_behind(): return lax.ppermute(block, axis, route)]
    ppermute x8 -> x0, waiting for transfers between devices: 49.9 us -> none  [from_behind(): return lax.ppermute(block, axis, route)]
    all_to_all x1 -> x0, waiting for transfers between devices: 36.4 us -> none  [on_device(): got = lax.all_to_all(packed, 'tm', split_axis=0, concat_axis=0, tiled=True)]
    dot_general x1 -> x2, matrix products: 5.34 us -> 16.7 us  [the longest x1 13.2 us: on_device(): jnp.dot(layer_norm(halo, norm_gain), weight[:, width:], preferred_element...]
    unnamed x18 -> x14, local copies, waits for them, and re-layouts: 22.6 us -> 13.8 us
  transfers between devices with their start and end apart: 10 -> 0, of which waited for: 5 -> 0; matrix products, arithmetic and copies ran while one was open for 4% -> 0% of each run, Pallas kernels for 0% -> 0%
where the time goes in v2:
time: 237 us; the launch traced here: 236 us
  Pallas kernels  127 us (54%)
  local copies, waits for them, and re-layouts  49.6 us (21%)
  matrix products  42.3 us (18%)
  other arithmetic  12.5 us (5%)
  loops' own time  3.64 us (2%)
    pallas_call x1, Pallas kernels, gather(): pl.pallas_call(functools.partial(gather_kernel, nx), out_shape=(jax.Shape...  88 us
    pallas_call x1, Pallas kernels, deal(): pl.pallas_call(functools.partial(deal_kernel, n), out_shape=jax.ShapeDtyp...  39 us
    unnamed x14, local copies, waits for them, and re-layouts  13.8 us
    reshape x1, local copies, waits for them, and re-layouts, on_device(): weight = gathered[:, :depth].reshape(n_tm * depth, columns)  13.7 us
    dot_general x1, matrix products, on_device(): jnp.dot(layer_norm(halo, norm_gain), weight[:, width:], preferred_element...  13.2 us
    sub x5, matrix products, attend(): raised = jnp.exp(scores - top)  12.9 us
    dot_general x5, matrix products, attend(): jnp.einsum('hqk,khd->qhd', probs, value_group, preferred_element_type=jnp...  11.8 us
    dynamic_slice x5, local copies, waits for them, and re-layouts, attend(): lax.dynamic_slice_in_dim(extended, start, span, 1).reshape(-1, group, HD)  6.89 us

profile of v2, /device:TPU:1, one launch (start us, length us, event | category | flops | bytes accessed | tf_op | source)
XLA Modules:
  0.0 235.9 jit_solution(14744226742566192774)
XLA Ops:
  0.7 0.7 convert_element_type.76
  1.4 0.7 fusion.62
  2.1 0.7 reshape.284
  2.8 1.6 pad_maximum_fusion.w_ref
  4.5 1.2 copy.43
  5.7 0.2 convert_reduce_fusion.1
  5.9 0.2 fusion.26
  6.1 88.0 %gather.1 = (bf16[64,21,3840]{2,1,0:T(8,128)(2,1)}, bf16[10,128,1280]{2,1,0:T(8,128)(2,1)}) custom-call(bf16[21,3840]{1,0:T(8,128)(2,1)} %pad_maximum_fusion.w_ref, bf16[128,1280]{1,0:T(8,128)(2,1)} %stem_ref.1), custom_call_target="tpu_custom_call" | custom-call | tf_op jit(solution)/shard_map/gather/pallas_call | solution.py:297
  94.1 2.9 %convert_reduce_fusion = f32[10,128]{1,0:T(8,128)S(1)} fusion(bf16[10,128,1280]{2,1,0:T(8,128)(2,1)} %get-tuple-element.81, pred[10]{0:T(512)(128)(4,1)S(1)} %compare_and_fusion), kind=kLoop, calls=%fused_computation.25 | loop fusion | flops 4913920 | bytes 3281930 | tf_op jit(solution)/shard_map/reduce_sum | solution.py:379
  96.9 1.2 multiply_reduce_fusion
  98.2 2.6 %fusion.13 = bf16[1280,1280]{1,0:T(8,128)(2,1)} fusion(f32[1280]{0:T(1024)S(1)} %copy-done.3, f32[1280]{0:T(1024)S(1)} %rsqrt_bitcast_fusion, f32[1280]{0:T(1024)S(1)} %get-tuple-element.160, bf16[10,128,1280]{2,1,0:T(8,128)(2,1)S(1)} %copy-done, pred[10]{0:T(512)(128)(4,1)S(1)} %compare_and_fusion), kind=kLoop, calls=%fused_computation.21 | loop fusion | flops 9830400 | bytes 6568970 | tf_op jit(solution)/shard_map/convert_element_type | solution.py:381
  100.8 3.1 %slice.44 = bf16[64,1,3840]{2,1,0:T(2,128)(2,1)S(1)} slice(bf16[64,21,3840]{2,1,0:T(8,128)(2,1)} %get-tuple-element.82), slice={[0:64], [20:21], [0:3840]} | slice | bytes 983040 | tf_op jit(solution)/shard_map/slice | solution.py:410
  104.1 0.2 compare_reduce_fusion
  104.4 0.6 reshape_reshape.3
  105.0 13.7 %reshape.287 = bf16[1280,3840]{1,0:T(8,128)(2,1)} reshape(bf16[64,20,3840]{2,1,0:T(8,128)(2,1)} %bitcast.103) | data formatting | bytes 19660800 | tf_op jit(solution)/shard_map/reshape | solution.py:409
  118.7 3.5 %fusion.16 = bf16[128,1280]{1,0:T(8,128)(2,1)} fusion(bf16[1280,3840]{1,0:T(8,128)(2,1)} %reshape.287, bf16[128,1280]{0,1:T(8,128)(2,1)S(1)} %copy.43, f32[1280]{0:T(1024)S(1)} %copy-done.3, f32[128]{0:T(128)S(1)} %add_rsqrt_fusion, f32[128]{0:T(128)S(1)} %broadcast_multiply_fusion.1), kind=kOutput, calls=%fused_computation.27 | convolution fusion | flops 420413440 | bytes 3938304 | tf_op jit(solution)/shard_map/dot_general | solution.py:422
  122.2 13.2 %convolution_convert_fusion = bf16[1280,2560]{1,0:T(8,128)(2,1)} fusion(bf16[1280,1280]{1,0:T(8,128)(2,1)S(1)} %copy-done.1, bf16[1280,3840]{1,0:T(8,128)(2,1)} %reshape.287), kind=kOutput, calls=%fused_computation.16 | convolution fusion | flops 8391884800 | bytes 16384000 | tf_op jit(solution)/shard_map/dot_general | solution.py:425
  135.4 9.5 %copy.44 = bf16[1280,2560]{0,1:T(8,128)(2,1)} copy(bf16[1280,2560]{1,0:T(8,128)(2,1)} %convolution_convert_fusion) | data formatting | bytes 13107200
  144.9 44.1 %while.13 = (s32[]{:T(128)}, f32[5,128,256]{1,2,0:T(8,128)S(1)}, s32[5]{0:T(128)S(1)}, bf16[1280,2560]{0,1:T(8,128)(2,1)}, bf16[128,1280]{1,0:T(8,128)(2,1)}, /*...) while((s32[]{:T(128)}, f32[5,128,256]{1,2,0:T(8,128)S(1)}, ...), condition=%wide.region_7.8_spmd.clone, body=%wide.region_4.7_spmd.clone.sunk | while | flops 171869440 | bytes 10233610 | solution.py:451
  144.9 0.6 dynamic_slice.47
  146.2 0.8 constant_dynamic-slice_fusion.6
  147.1 0.2 broadcast_compare_fusion.2
  147.3 1.4 constant_dynamic-slice_fusion.5
  148.7 2.6 %fusion.83 = (f32[4,128]{1,0:T(4,128)S(1)}, f32[4,128,1280]{2,1,0:T(8,128)}) fusion(bf16[128,4,64]{0,2,1:T(8,128)(2,1)S(1)} %bitcast.111, bf16[1280,4,64]{0,2,1:T(8,128)(2,1)S(1)} %bitcast.102, pred[128,1280]{1,0:T(8,128)(4,1)S(1)} %broadcast_compare_fusion.2), kind=kOutput, calls=%fused_computation.115.clone.1 | convolution fusion | flops 86508800 | bytes 3508224 | tf_op jit(solution)/shard_map/while/body/eval_jaxpr/sub | solution.py:446
  151.3 2.4 fusion.84
  153.7 0.6 dynamic_slice.47
  154.9 0.8 constant_dynamic-slice_fusion.6
  155.9 0.2 broadcast_compare_fusion.2
  156.1 1.4 constant_dynamic-slice_fusion.5
  157.5 2.6 %fusion.83 = (f32[4,128]{1,0:T(4,128)S(1)}, f32[4,128,1280]{2,1,0:T(8,128)}) fusion(bf16[128,4,64]{0,2,1:T(8,128)(2,1)S(1)} %bitcast.111, bf16[1280,4,64]{0,2,1:T(8,128)(2,1)S(1)} %bitcast.102, pred[128,1280]{1,0:T(8,128)(4,1)S(1)} %broadcast_compare_fusion.2), kind=kOutput, calls=%fused_computation.115.clone.1 | convolution fusion | flops 86508800 | bytes 3508224 | tf_op jit(solution)/shard_map/while/body/eval_jaxpr/sub | solution.py:446
  160.1 2.4 fusion.84
  162.5 0.6 dynamic_slice.47
  163.7 0.8 constant_dynamic-slice_fusion.6
  164.7 0.2 broadcast_compare_fusion.2
  164.9 1.4 constant_dynamic-slice_fusion.5
  166.2 2.6 %fusion.83 = (f32[4,128]{1,0:T(4,128)S(1)}, f32[4,128,1280]{2,1,0:T(8,128)}) fusion(bf16[128,4,64]{0,2,1:T(8,128)(2,1)S(1)} %bitcast.111, bf16[1280,4,64]{0,2,1:T(8,128)(2,1)S(1)} %bitcast.102, pred[128,1280]{1,0:T(8,128)(4,1)S(1)} %broadcast_compare_fusion.2), kind=kOutput, calls=%fused_computation.115.clone.1 | convolution fusion | flops 86508800 | bytes 3508224 | tf_op jit(solution)/shard_map/while/body/eval_jaxpr/sub | solution.py:446
  168.8 2.4 fusion.84
  171.3 0.6 dynamic_slice.47
  172.5 0.8 constant_dynamic-slice_fusion.6
  173.5 0.2 broadcast_compare_fusion.2
  173.7 1.4 constant_dynamic-slice_fusion.5
  175.0 2.6 %fusion.83 = (f32[4,128]{1,0:T(4,128)S(1)}, f32[4,128,1280]{2,1,0:T(8,128)}) fusion(bf16[128,4,64]{0,2,1:T(8,128)(2,1)S(1)} %bitcast.111, bf16[1280,4,64]{0,2,1:T(8,128)(2,1)S(1)} %bitcast.102, pred[128,1280]{1,0:T(8,128)(4,1)S(1)} %broadcast_compare_fusion.2), kind=kOutput, calls=%fused_computation.115.clone.1 | convolution fusion | flops 86508800 | bytes 3508224 | tf_op jit(solution)/shard_map/while/body/eval_jaxpr/sub | solution.py:446
  177.6 2.4 fusion.84
  180.0 0.6 dynamic_slice.47
  181.3 0.8 constant_dynamic-slice_fusion.6
  182.3 0.2 broadcast_compare_fusion.2
  182.4 1.4 constant_dynamic-slice_fusion.5
  183.8 2.6 %fusion.83 = (f32[4,128]{1,0:T(4,128)S(1)}, f32[4,128,1280]{2,1,0:T(8,128)}) fusion(bf16[128,4,64]{0,2,1:T(8,128)(2,1)S(1)} %bitcast.111, bf16[1280,4,64]{0,2,1:T(8,128)(2,1)S(1)} %bitcast.102, pred[128,1280]{1,0:T(8,128)(4,1)S(1)} %broadcast_compare_fusion.2), kind=kOutput, calls=%fused_computation.115.clone.1 | convolution fusion | flops 86508800 | bytes 3508224 | tf_op jit(solution)/shard_map/while/body/eval_jaxpr/sub | solution.py:446
  186.4 2.4 fusion.84
  189.1 0.9 copy.58
  190.0 0.6 fusion.68
  190.6 0.3 fusion.19
  190.9 0.2 fusion.20
  191.3 0.2 copy.53
  191.5 0.1 reshape.293
  191.6 0.4 copy.48
  192.1 0.5 reshape.292
  192.6 0.9 copy.64
  193.5 39.0 %deal.1 = bf16[64,32,128]{2,1,0:T(8,128)(2,1)} custom-call(bf16[64,32,128]{2,1,0:T(8,128)(2,1)} %bitcast.110), custom_call_target="tpu_custom_call" | custom-call | tf_op jit(solution)/shard_map/deal/pallas_call | solution.py:366
  232.5 1.2 copy.72
  233.9 0.2 fusion.44
  234.3 0.5 mul.95
  234.8 0.4 mul.96
  235.3 0.6 divide_convert_fusion.2
  (54 shorter events, 2.0 us)
Async XLA Ops:
  94.0 2.9 %copy-start = (bf16[10,128,1280]{2,1,0:T(8,128)(2,1)S(1)}, bf16[10,128,1280]{2,1,0:T(8,128)(2,1)}, u32[]{:S(2)}) copy-start(bf16[10,128,1280]{2,1,0:T(8,128)(2,1)} %get-tuple-element.81) | copy-start | bytes 9830404
  94.0 4.1 %copy-start.3 = (f32[1280]{0:T(1024)S(1)}, f32[1280]{0:T(1024)}, u32[]{:S(2)}) copy-start(f32[1280]{0:T(1024)} %param.9) | copy-start | bytes 15364
  118.7 3.5 %copy-start.1 = (bf16[1280,1280]{1,0:T(8,128)(2,1)S(1)}, bf16[1280,1280]{1,0:T(8,128)(2,1)}, u32[]{:S(2)}) copy-start(bf16[1280,1280]{1,0:T(8,128)(2,1)} %fusion.13) | copy-start | bytes 9830404
  135.4 9.5 %copy-start.2 = (s32[128]{0:T(128)S(1)}, s32[128]{0:T(128)}, u32[]{:S(2)}) copy-start(s32[128]{0:T(128)} %param.11) | copy-start | bytes 1540

commit v3 on v2

--- a/solution.py
+++ b/solution.py
@@ -1,5 +1,4 @@
 import functools
-import math
 
 import jax
 import jax.numpy as jnp
@@ -374,6 +373,74 @@
     )(payload)
 
 
+def encode_kernel(heads_step, own_ref, halo_ref, exists_ref, wq_ref, wk_ref, wv_ref, bias_ref, stem_ref, out_ref, clean):
+    @pl.when(pl.program_id(0) == 0)
+    def _():
+        clean[...] = jnp.where(exists_ref[...] > 0, halo_ref[...], jnp.bfloat16(0))
+
+    def project(rows, w_ref):
+        return jnp.dot(rows, w_ref[...], preferred_element_type=jnp.float32).astype(jnp.bfloat16)
+
+    query = project(own_ref[...], wq_ref) * jnp.bfloat16(HD ** (-0.5))
+    key = project(clean[...], wk_ref)
+    value = project(clean[...], wv_ref)
+    pair = 2 * HD
+    low = lax.broadcasted_iota(jnp.int32, (query.shape[0], pair), 1) < HD
+    for p in range(heads_step // 2):
+        at = slice(p * pair, (p + 1) * pair)
+        parts = []
+        for h in range(2):
+            mine = low if h == 0 else jnp.logical_not(low)
+            scores = lax.dot_general(
+                jnp.where(mine, query[:, at], jnp.bfloat16(0)),
+                key[:, at],
+                (((1,), (1,)), ((), ())),
+                preferred_element_type=jnp.float32,
+            )
+            scores = scores + bias_ref[...]
+            raised = jnp.exp(scores - jnp.max(scores, axis=-1, keepdims=True))
+            total = jnp.sum(raised, axis=-1, keepdims=True)
+            probs = (raised * (1.0 / total)).astype(jnp.bfloat16)
+            parts.append(jnp.dot(probs, value[:, at], preferred_element_type=jnp.float32))
+        context = jnp.where(low, parts[0], parts[1])
+        out_ref[:, at] = (stem_ref[:, at].astype(jnp.float32) + context).astype(jnp.bfloat16)
+
+
+def encode(own, halo, exists, weight, bias, stem):
+    rows, width = stem.shape
+    depth = own.shape[1]
+    around = halo.shape[0]
+    heads_step = 4
+    span = heads_step * HD
+    steps = width // span
+
+    def whole(*shape):
+        return pl.BlockSpec(shape, lambda i: (0,) * len(shape))
+
+    def columns(first):
+        return pl.BlockSpec((depth, span), lambda i: (0, first * steps + i))
+
+    piece = pl.BlockSpec((rows, span), lambda i: (0, i))
+    return pl.pallas_call(
+        functools.partial(encode_kernel, heads_step),
+        grid=(steps,),
+        out_shape=jax.ShapeDtypeStruct(stem.shape, stem.dtype),
+        in_specs=[
+            whole(rows, depth),
+            whole(around, depth),
+            whole(around, 1),
+            columns(0),
+            columns(1),
+            columns(2),
+            whole(rows, around),
+            piece,
+        ],
+        out_specs=piece,
+        scratch_shapes=[pltpu.VMEM((around, depth), jnp.bfloat16)],
+        name="encode",
+    )(own, halo, exists, weight, weight, weight, bias, stem)
+
+
 def layer_norm(block, gain):
     values_in = block.astype(jnp.float32)
     mean = jnp.mean(values_in, axis=-1, keepdims=True)
@@ -404,10 +471,16 @@
     cuts = [tokens_dev * width, tokens_dev * (width + n_tm)]
     cuts += [cuts[1] + rows, cuts[1] + 2 * rows]
     depth, columns = qkv_weight.shape
-    small = jnp.pad(small, (0, -cuts[3] % columns)).reshape(-1, columns)
-    gathered, halo = gather(jnp.concatenate([qkv_weight, small], axis=0), stem, n_tm)
-    weight = gathered[:, :depth].reshape(n_tm * depth, columns)
-    small_all = gathered[:, depth:].reshape(n_tm, -1)
+    padded = depth + 1 + (-(depth + 1) % 8)
+    spread_at = (jnp.arange(width) // depth) * padded + jnp.arange(width) % depth
+    spread = (spread_at[:, None] == jnp.arange(n_tm * padded)[None, :]).astype(jnp.bfloat16)
+    own = jnp.dot(
+        layer_norm(stem, norm_gain), spread, preferred_element_type=jnp.float32
+    ).astype(jnp.bfloat16)
+    small = jnp.pad(small, (0, (padded - depth) * columns - cuts[3])).reshape(-1, columns)
+    gathered, halo = gather(jnp.concatenate([qkv_weight, small], axis=0), own, n_tm)
+    weight = gathered.reshape(n_tm * padded, columns)
+    small_all = gathered[:, depth]
     all_queries = small_all[:, : cuts[0]].reshape(n_tm * tokens_dev, width)
     all_masks = small_all[:, cuts[0] : cuts[1]].reshape(n_tm * tokens_dev, n_tm)
     seg_low = small_all[:, cuts[1] : cuts[2]].reshape(-1).astype(jnp.int32)
@@ -418,39 +491,10 @@
     seg_wide = lax.dynamic_slice_in_dim(seg_all, chip * 2 * rows, around * rows, 0)
     block_at = chip * 2 - 2 * REACH + jnp.arange(around, dtype=jnp.int32)
     exists = (block_at >= 0) & (block_at < n_tm)
-    halo = jnp.where(exists[:, None, None], halo, jnp.bfloat16(0)).reshape(around * rows, width)
-    query_part = jnp.dot(
-        layer_norm(stem, norm_gain), weight[:, :width], preferred_element_type=jnp.float32
-    ).astype(jnp.bfloat16)
-    extended = jnp.dot(
-        layer_norm(halo, norm_gain), weight[:, width:], preferred_element_type=jnp.float32
-    ).astype(jnp.bfloat16)
+    exists = jnp.repeat(exists.astype(jnp.int32), rows)[:, None]
     same = segment_ids[:, None] == seg_wide[None, :]
-    group = math.gcd(heads, 4)
-    span = group * HD
-    groups = heads // group
-
-    def attend(index):
-        start = index * span
-        query_group = lax.dynamic_slice_in_dim(query_part, start, span, 1).reshape(rows, group, HD)
-        key_group = lax.dynamic_slice_in_dim(extended, start, span, 1).reshape(-1, group, HD)
-        value_group = lax.dynamic_slice_in_dim(extended, width + start, span, 1).reshape(
-            -1, group, HD
-        )
-        scores = (
-            jnp.einsum("qhd,khd->hqk", query_group, key_group, preferred_element_type=jnp.float32)
-            * scale
-        )
-        scores = jnp.where(same[None], scores, jnp.float32(-1e30))
-        top = jnp.max(scores, axis=-1, keepdims=True)
-        raised = jnp.exp(scores - top)
-        probs = (raised / jnp.sum(raised, axis=-1, keepdims=True)).astype(jnp.bfloat16)
-        context = jnp.einsum("hqk,khd->qhd", probs, value_group, preferred_element_type=jnp.float32)
-        return context.reshape(rows, span)
-
-    contexts = lax.map(attend, jnp.arange(groups, dtype=jnp.int32))
-    context = jnp.transpose(contexts, (1, 0, 2)).reshape(rows, width)
-    memory = (stem.astype(jnp.float32) + context).astype(jnp.bfloat16)
+    bias = jnp.where(same, jnp.float32(0.0), jnp.float32(-1e30))
+    memory = encode(own, halo.reshape(around * rows, -1), exists, weight, bias, stem)
     total_tokens = all_queries.shape[0]
     column = lax.dynamic_slice_in_dim(all_masks, device, 1, 1)[:, 0]
     owner = jnp.arange(total_tokens, dtype=jnp.int32) // tokens_dev

time: 237 us -> 182 us (0.77)
  local copies, waits for them, and re-layouts: 49.6 us -> 11.1 us
  matrix products: 42.3 us -> 4.57 us
  Pallas kernels: 127 us -> 159 us
  other arithmetic: 12.5 us -> 5.55 us
  loops' own time: 3.64 us -> 0 us
    pallas_call x0 -> x1, Pallas kernels: none -> 26.5 us  [encode(): pl.pallas_call(functools.partial(encode_kernel, heads_step), grid=(steps,...]
    dot_general x7 -> x1, matrix products: 28.4 us -> 3.65 us  [on_device(): jnp.dot(layer_norm(stem, norm_gain), spread, preferred_element_type=jnp.f...]
    dynamic_slice x20 -> x0, local copies, waits for them, and re-layouts: 14.7 us -> none  [the longest x5 6.89 us: attend(): lax.dynamic_slice_in_dim(extended, start, span, 1).reshape(-1, group, HD)]
    reshape x2 -> x1, local copies, waits for them, and re-layouts: 13.7 us -> 0.02 us  [on_device(): jnp.pad(small, (0, (padded - depth) * columns - cuts[3]))]
    sub x5 -> x0, matrix products: 12.9 us -> none  [attend(): raised = jnp.exp(scores - top)]
    unnamed x14, local copies, waits for them, and re-layouts: 13.8 us -> 3.38 us
    pallas_call x1, Pallas kernels: 88 us -> 94.6 us  [gather(): pl.pallas_call(functools.partial(gather_kernel, nx), out_shape=(jax.Shape...]
    another operation x1 -> x0, loops' own time: 3.64 us -> none  [on_device(): contexts = lax.map(attend, jnp.arange(groups, dtype=jnp.int32))]
where the time goes in v3:
time: 182 us; the launch traced here: 181 us
  Pallas kernels  159 us (87%)
  local copies, waits for them, and re-layouts  11.1 us (6%)
  other arithmetic  5.55 us (3%)
  matrix products  4.57 us (3%)
    pallas_call x1, Pallas kernels, gather(): pl.pallas_call(functools.partial(gather_kernel, nx), out_shape=(jax.Shape...  94.6 us
    pallas_call x1, Pallas kernels, deal(): pl.pallas_call(functools.partial(deal_kernel, n), out_shape=jax.ShapeDtyp...  38.2 us
    pallas_call x1, Pallas kernels, encode(): pl.pallas_call(functools.partial(encode_kernel, heads_step), grid=(steps,...  26.5 us
    dot_general x1, matrix products, on_device(): jnp.dot(layer_norm(stem, norm_gain), spread, preferred_element_type=jnp.f...  3.65 us

profile of v3, /device:TPU:1, one launch (start us, length us, event | category | flops | bytes accessed | tf_op | source)
XLA Modules:
  0.0 181.5 jit_solution(7012984651361666322)
XLA Ops:
  0.6 1.1 convert_reduce_fusion
  1.8 1.2 fusion.10
  3.0 0.0 copy-start.2
  3.0 0.0 copy-start.1
  3.0 0.0 copy-start.3
  3.0 0.0 copy-start
  3.0 3.6 %fusion.2.stem_ref.own_ref = bf16[128,1536]{1,0:T(8,128)(2,1)} fusion(s32[1280]{0:T(1024)S(1)} %fusion.51, bf16[128,1280]{1,0:T(8,128)(2,1)} %stem_ref.1, f32[1280]{0:T(1024)} %param.7, f32[128]{0:T(128)S(1)} %add_rsqrt_fusion, f32[128]{0:T(128)S(1)} %broadcast_multiply_fusion), kind=kOutput, calls=%fused_computation.3 | convolution fusion | flops 506298368 | bytes 732160 | tf_op jit(solution)/shard_map/dot_general | solution.py:477
  6.7 0.0 copy-done.2
  6.7 0.0 copy-done.1
  6.7 0.0 copy-done.3
  6.8 0.1 reshape.235
  6.9 0.0 copy-done
  6.9 0.7 pad_maximum_fusion.w_ref
  7.6 94.6 %gather.1 = (bf16[64,24,3840]{2,1,0:T(8,128)(2,1)}, bf16[10,128,1536]{2,1,0:T(8,128)(2,1)}) custom-call(bf16[24,3840]{1,0:T(8,128)(2,1)} %pad_maximum_fusion.w_ref, bf16[128,1536]{1,0:T(8,128)(2,1)} %fusion.2.stem_ref.own_ref), custom_call_target="tpu_custom_call" | custom-call | tf_op jit(solution)/shard_map/gather/pallas_call | solution.py:296
  102.2 3.1 %slice.33 = bf16[64,1,3840]{2,1,0:T(2,128)(2,1)S(1)} slice(bf16[64,24,3840]{2,1,0:T(8,128)(2,1)} %get-tuple-element.5), slice={[0:64], [20:21], [0:3840]} | slice | bytes 983040 | tf_op jit(solution)/shard_map/slice | solution.py:483
  105.3 0.1 copy.66
  105.4 0.1 pad_dynamic-slice_fusion
  105.5 1.0 compare_select_fusion.bias_ref
  106.4 0.1 broadcast_bitcast_fusion
  106.5 1.1 copy.55
  107.6 26.5 %encode.1 = bf16[128,1280]{1,0:T(8,128)(2,1)} custom-call(bf16[128,1536]{1,0:T(8,128)(2,1)} %fusion.2.stem_ref.own_ref, bf16[1280,1536]{1,0:T(8,128)(2,1)} %bitcast.69, s32[1280,1]{1,0:T(8,128)} %bitcast.74, bf16[1536,3840]{1,0:T(8,128)(2,1)} %bitcast.66, bf16[1536,3840]{1,0:T(8,128)(2,1)} %bitcast.67, bf16[1536,3840]{1,0:T(8,128)(2,1)} %bitcast.68, ...), custom_call_target="tpu_custom_call" | custom-call | tf_op jit(solution)/shard_map/encode/pallas_call | solution.py:424
  134.2 1.2 copy.37
  135.4 0.6 reshape_reshape.3
  136.0 0.6 fusion.58
  136.6 0.1 reshape.240
  136.7 0.2 compare_reduce_fusion
  136.9 0.3 fusion.3
  137.2 0.4 copy.40
  137.7 0.5 reshape.241
  138.2 0.2 fusion.4
  138.5 0.1 maximum_bitcast_fusion
  138.5 0.2 copy.45
  138.7 0.1 reshape.242
  138.9 0.9 copy.56
  139.8 38.2 %deal.1 = bf16[64,32,128]{2,1,0:T(8,128)(2,1)} custom-call(bf16[64,32,128]{2,1,0:T(8,128)(2,1)} %bitcast.76), custom_call_target="tpu_custom_call" | custom-call | tf_op jit(solution)/shard_map/deal/pallas_call | solution.py:365
  178.1 1.2 copy.65
  179.3 0.1 copy.46
  179.4 0.1 fusion.53
  179.5 0.2 fusion.34
  179.7 0.1 copy.49
  179.8 0.5 mul.72
  180.2 0.4 mul.73
  180.6 0.1 fusion.14
  180.7 0.1 div.62
  180.8 0.1 div.63
  180.9 0.6 divide_convert_fusion
  (25 shorter events, 0.3 us)
Async XLA Ops:
  3.0 3.7 %copy-start.2 = (s32[128]{0:T(128)S(1)}, s32[128]{0:T(128)}, u32[]{:S(2)}) copy-start(s32[128]{0:T(128)} %param.9) | copy-start | bytes 1540
  3.0 3.7 %copy-start.1 = (bf16[2,1280]{1,0:T(2,128)(2,1)S(1)}, bf16[2,1280]{1,0:T(2,128)(2,1)}, u32[]{:S(2)}) copy-start(bf16[2,1280]{1,0:T(2,128)(2,1)} %param.10) | copy-start | bytes 15364
  3.0 3.7 %copy-start.3 = (s32[2,64]{1,0:T(2,128)S(1)}, s32[2,64]{1,0:T(2,128)}, u32[]{:S(2)}) copy-start(s32[2,64]{1,0:T(2,128)} %param.11) | copy-start | bytes 1540
  3.0 3.9 %copy-start = (bf16[20,3840]{1,0:T(8,128)(2,1)S(1)}, bf16[20,3840]{1,0:T(8,128)(2,1)}, u32[]{:S(2)}) copy-start(bf16[20,3840]{1,0:T(8,128)(2,1)} %param.8) | copy-start | bytes 460804

commit v4 on v3

--- a/solution.py
+++ b/solution.py
@@ -113,14 +113,6 @@
     def _():
         to_down(z, True).start()
 
-    @pl.when(has_next)
-    def _():
-        h_next.start()
-
-    @pl.when(has_prev)
-    def _():
-        h_prev.start()
-
     to_right(x, z, 0, True).start()
     to_left(x, z, 0, True).start()
     to_partner(x, z, True).start()
@@ -191,6 +183,16 @@
 
     lax.fori_loop(1, 4, step, 0)
 
+    @pl.when(has_next)
+    def _():
+        h_next.start()
+
+    @pl.when(has_prev)
+    def _():
+        h_prev.start()
+
+    lax.fori_loop(4, NZ, step, 0)
+
     @pl.when(has_prev)
     def _():
         h_arrived(slot_of(-1, core))
@@ -209,7 +211,7 @@
         def _():
             relay_prev.start()
 
-    lax.fori_loop(4, NZ + 2, step, 0)
+    lax.fori_loop(NZ, NZ + 2, step, 0)
 
     @pl.when(chip >= 2)
     def _():
@@ -522,7 +524,7 @@
     stats = jnp.stack([top_high, top_low, den_high, den_low]).astype(jnp.bfloat16)
     stats = jnp.transpose(stats, (2, 0, 1)).reshape(n_tm, -1)
     payload = jnp.concatenate([numer.reshape(n_tm, -1), stats], axis=1)
-    payload = jnp.pad(payload, ((0, 0), (0, -payload.shape[1] % 2048)))
+    payload = jnp.pad(payload, ((0, 0), (0, -payload.shape[1] % 1024)))
     got = deal(payload.reshape(n_tm, -1, 128)).reshape(n_tm, -1).astype(jnp.float32)
     num_all = got[:, : tokens_dev * width].reshape(n_tm, tokens_dev, heads, HD)
     stats = got[:, tokens_dev * width : tokens_dev * (width + 4 * heads)]

time: 182 us -> 175 us (0.962)
  Pallas kernels: 159 us -> 153 us
    pallas_call x1, Pallas kernels: 94.6 us -> 90.4 us  [gather(): pl.pallas_call(functools.partial(gather_kernel, nx), out_shape=(jax.Shape...]
    pallas_call x1, Pallas kernels: 38.2 us -> 35.7 us  [deal(): pl.pallas_call(functools.partial(deal_kernel, n), out_shape=jax.ShapeDtyp...]
where the time goes in v4:
time: 175 us
  Pallas kernels  153 us (87%)
  local copies, waits for them, and re-layouts  10.8 us (6%)
  other arithmetic  5.54 us (3%)
  matrix products  4.57 us (3%)
    pallas_call x1, Pallas kernels, gather(): pl.pallas_call(functools.partial(gather_kernel, nx), out_shape=(jax.Shape...  90.4 us
    pallas_call x1, Pallas kernels, deal(): pl.pallas_call(functools.partial(deal_kernel, n), out_shape=jax.ShapeDtyp...  35.7 us
    pallas_call x1, Pallas kernels, encode(): pl.pallas_call(functools.partial(encode_kernel, heads_step), grid=(steps,...  26.5 us
    dot_general x1, matrix products, on_device(): jnp.dot(layer_norm(stem, norm_gain), spread, preferred_element_type=jnp.f...  3.65 us

profile of v4, /device:TPU:1, one launch (start us, length us, event | category | flops | bytes accessed | tf_op | source)
XLA Modules:
  0.0 174.5 jit_solution(3879731045587343820)
XLA Ops:
  0.6 1.1 convert_reduce_fusion
  1.8 1.2 fusion.10
  3.0 0.0 copy-start.2
  3.0 0.0 copy-start.1
  3.0 0.0 copy-start.3
  3.0 0.0 copy-start
  3.0 3.6 %fusion.2.stem_ref.own_ref = bf16[128,1536]{1,0:T(8,128)(2,1)} fusion(s32[1280]{0:T(1024)S(1)} %fusion.51, bf16[128,1280]{1,0:T(8,128)(2,1)} %stem_ref.1, f32[1280]{0:T(1024)} %param.7, f32[128]{0:T(128)S(1)} %add_rsqrt_fusion, f32[128]{0:T(128)S(1)} %broadcast_multiply_fusion), kind=kOutput, calls=%fused_computation.3 | convolution fusion | flops 506298368 | bytes 732160 | tf_op jit(solution)/shard_map/dot_general | solution.py:479
  6.7 0.0 copy-done.2
  6.7 0.0 copy-done.1
  6.7 0.0 copy-done.3
  6.8 0.1 reshape.235
  6.9 0.0 copy-done
  6.9 0.7 pad_maximum_fusion.w_ref
  7.6 90.4 %gather.1 = (bf16[64,24,3840]{2,1,0:T(8,128)(2,1)}, bf16[10,128,1536]{2,1,0:T(8,128)(2,1)}) custom-call(bf16[24,3840]{1,0:T(8,128)(2,1)} %pad_maximum_fusion.w_ref, bf16[128,1536]{1,0:T(8,128)(2,1)} %fusion.2.stem_ref.own_ref), custom_call_target="tpu_custom_call" | custom-call | tf_op jit(solution)/shard_map/gather/pallas_call | solution.py:298
  98.0 3.1 %slice.33 = bf16[64,1,3840]{2,1,0:T(2,128)(2,1)S(1)} slice(bf16[64,24,3840]{2,1,0:T(8,128)(2,1)} %get-tuple-element.5), slice={[0:64], [20:21], [0:3840]} | slice | bytes 983040 | tf_op jit(solution)/shard_map/slice | solution.py:485
  101.1 0.1 copy.66
  101.2 0.1 pad_dynamic-slice_fusion
  101.3 1.0 compare_select_fusion.bias_ref
  102.3 0.1 broadcast_bitcast_fusion
  102.3 1.1 copy.55
  103.5 26.5 %encode.1 = bf16[128,1280]{1,0:T(8,128)(2,1)} custom-call(bf16[128,1536]{1,0:T(8,128)(2,1)} %fusion.2.stem_ref.own_ref, bf16[1280,1536]{1,0:T(8,128)(2,1)} %bitcast.69, s32[1280,1]{1,0:T(8,128)} %bitcast.74, bf16[1536,3840]{1,0:T(8,128)(2,1)} %bitcast.66, bf16[1536,3840]{1,0:T(8,128)(2,1)} %bitcast.67, bf16[1536,3840]{1,0:T(8,128)(2,1)} %bitcast.68, ...), custom_call_target="tpu_custom_call" | custom-call | tf_op jit(solution)/shard_map/encode/pallas_call | solution.py:426
  130.0 1.2 copy.37
  131.2 0.6 reshape_reshape.3
  131.8 0.6 fusion.58
  132.5 0.1 reshape.240
  132.5 0.2 compare_reduce_fusion
  132.7 0.3 fusion.3
  133.1 0.4 copy.40
  133.5 0.5 reshape.241
  134.0 0.2 fusion.4
  134.3 0.1 maximum_bitcast_fusion
  134.4 0.2 copy.45
  134.5 0.1 reshape.242
  134.7 0.8 copy.56
  135.5 35.7 %deal.1 = bf16[64,24,128]{2,1,0:T(8,128)(2,1)} custom-call(bf16[64,24,128]{2,1,0:T(8,128)(2,1)} %bitcast.75), custom_call_target="tpu_custom_call" | custom-call | tf_op jit(solution)/shard_map/deal/pallas_call | solution.py:367
  171.2 1.0 copy.65
  172.3 0.1 copy.46
  172.4 0.1 fusion.53
  172.5 0.2 fusion.34
  172.7 0.1 copy.49
  172.8 0.5 mul.72
  173.3 0.4 mul.73
  173.7 0.1 fusion.14
  173.8 0.1 div.62
  173.8 0.1 div.63
  173.9 0.6 divide_convert_fusion
  (25 shorter events, 0.3 us)
Async XLA Ops:
  3.0 3.7 %copy-start.2 = (s32[128]{0:T(128)S(1)}, s32[128]{0:T(128)}, u32[]{:S(2)}) copy-start(s32[128]{0:T(128)} %param.9) | copy-start | bytes 1540
  3.0 3.7 %copy-start.1 = (bf16[2,1280]{1,0:T(2,128)(2,1)S(1)}, bf16[2,1280]{1,0:T(2,128)(2,1)}, u32[]{:S(2)}) copy-start(bf16[2,1280]{1,0:T(2,128)(2,1)} %param.10) | copy-start | bytes 15364
  3.0 3.7 %copy-start.3 = (s32[2,64]{1,0:T(2,128)S(1)}, s32[2,64]{1,0:T(2,128)}, u32[]{:S(2)}) copy-start(s32[2,64]{1,0:T(2,128)} %param.11) | copy-start | bytes 1540
  3.0 3.9 %copy-start = (bf16[20,3840]{1,0:T(8,128)(2,1)S(1)}, bf16[20,3840]{1,0:T(8,128)(2,1)}, u32[]{:S(2)}) copy-start(bf16[20,3840]{1,0:T(8,128)(2,1)} %param.8) | copy-start | bytes 460804

commit v5 on v4

--- a/solution.py
+++ b/solution.py
@@ -13,7 +13,7 @@
 MESH = pl.DeviceIdType.MESH
 
 
-def gather_kernel(nx, w_ref, stem_ref, wide_ref, halo_ref, w_recv, w_zs, w_xs, w_ps, h_recv, h_zs, h_ps, own_sem):
+def gather_kernel(nx, w_ref, stem_ref, gain_ref, at_ref, wide_ref, halo_ref, own_ref, w_recv, w_zs, w_xs, w_ps, h_recv, h_zs, h_ps, own_sem):
     me = lax.axis_index("tm")
     core = lax.rem(me, 2)
     chip = me // 2
@@ -62,7 +62,7 @@
 
     def h_copy(from_slot, to_slot, peer, send_sem, own=False):
         return pltpu.make_async_remote_copy(
-            src_ref=stem_ref if own else halo_ref.at[from_slot],
+            src_ref=own_ref if own else halo_ref.at[from_slot],
             dst_ref=halo_ref.at[to_slot],
             send_sem=send_sem,
             recv_sem=h_recv.at[to_slot],
@@ -116,11 +116,15 @@
     to_right(x, z, 0, True).start()
     to_left(x, z, 0, True).start()
     to_partner(x, z, True).start()
-    h_own.start()
     own_w = pltpu.make_async_copy(w_ref, wide_ref.at[me], own_sem.at[0])
-    own_h = pltpu.make_async_copy(stem_ref, halo_ref.at[own_slot], own_sem.at[1])
+    own_h = pltpu.make_async_copy(own_ref, halo_ref.at[own_slot], own_sem.at[1])
     own_w.start()
-    own_h.start()
+
+    lanes = lax.broadcasted_iota(jnp.int32, (at_ref.shape[0], own_ref.shape[1]), 1)
+    spread = jnp.where(lanes == at_ref[...], 1.0, 0.0).astype(jnp.bfloat16)
+    own_ref[...] = jnp.dot(
+        layer_norm(stem_ref[...], gain_ref[...]), spread, preferred_element_type=jnp.float32
+    ).astype(jnp.bfloat16)
 
     def beside(zz, fresh):
         ok = (zz >= 0) & (zz < NZ) & fresh
@@ -183,6 +187,9 @@
 
     lax.fori_loop(1, 4, step, 0)
 
+    h_own.start()
+    own_h.start()
+
     @pl.when(has_next)
     def _():
         h_next.start()
@@ -292,18 +299,20 @@
     own_h.wait()
 
 
-def gather(wide, stem, n_tm):
+def gather(wide, stem, gain, spread_at, n_tm):
     nx = n_tm // (2 * NZ)
+    own = (stem.shape[0], n_tm * wide.shape[0])
     dma = pltpu.SemaphoreType.DMA
     return pl.pallas_call(
         functools.partial(gather_kernel, nx),
         out_shape=(
             jax.ShapeDtypeStruct((n_tm, *wide.shape), wide.dtype),
-            jax.ShapeDtypeStruct((4 * REACH + 2, *stem.shape), stem.dtype),
+            jax.ShapeDtypeStruct((4 * REACH + 2, *own), stem.dtype),
         ),
-        in_specs=[pl.BlockSpec(memory_space=pltpu.VMEM)] * 2,
+        in_specs=[pl.BlockSpec(memory_space=pltpu.VMEM)] * 4,
         out_specs=(pl.BlockSpec(memory_space=pl.ANY), pl.BlockSpec(memory_space=pl.ANY)),
         scratch_shapes=[
+            pltpu.VMEM(own, stem.dtype),
             dma((n_tm,)),
             dma((2, NZ)),
             dma((2, 2 * NZ)),
@@ -315,7 +324,7 @@
         ],
         compiler_params=pltpu.CompilerParams(collective_id=0, has_side_effects=True),
         name="gather",
-    )(wide, stem)
+    )(wide, stem, gain, spread_at)
 
 
 def deal_kernel(n, out_ref, in_ref, send_sem, recv_sem, own_sem):
@@ -375,15 +384,19 @@
     )(payload)
 
 
-def encode_kernel(heads_step, own_ref, halo_ref, exists_ref, wq_ref, wk_ref, wv_ref, bias_ref, stem_ref, out_ref, clean):
+def encode_kernel(heads_step, halo_ref, exists_ref, wq_ref, wk_ref, wv_ref, bias_ref, stem_ref, out_ref, clean):
+    rows = out_ref.shape[0]
+
     @pl.when(pl.program_id(0) == 0)
     def _():
-        clean[...] = jnp.where(exists_ref[...] > 0, halo_ref[...], jnp.bfloat16(0))
-
-    def project(rows, w_ref):
-        return jnp.dot(rows, w_ref[...], preferred_element_type=jnp.float32).astype(jnp.bfloat16)
-
-    query = project(own_ref[...], wq_ref) * jnp.bfloat16(HD ** (-0.5))
+        first = lax.rem(lax.axis_index("tm"), 2) * rows
+        near = halo_ref[pl.ds(pl.multiple_of(first, rows), clean.shape[0]), :]
+        clean[...] = jnp.where(exists_ref[...] > 0, near, jnp.bfloat16(0))
+
+    def project(block, w_ref):
+        return jnp.dot(block, w_ref[...], preferred_element_type=jnp.float32).astype(jnp.bfloat16)
+
+    query = project(clean[2 * REACH * rows : (2 * REACH + 1) * rows, :], wq_ref) * jnp.bfloat16(HD ** (-0.5))
     key = project(clean[...], wk_ref)
     value = project(clean[...], wv_ref)
     pair = 2 * HD
@@ -408,10 +421,10 @@
         out_ref[:, at] = (stem_ref[:, at].astype(jnp.float32) + context).astype(jnp.bfloat16)
 
 
-def encode(own, halo, exists, weight, bias, stem):
+def encode(halo, exists, weight, bias, stem):
     rows, width = stem.shape
-    depth = own.shape[1]
-    around = halo.shape[0]
+    depth = halo.shape[1]
+    around = bias.shape[1]
     heads_step = 4
     span = heads_step * HD
     steps = width // span
@@ -428,8 +441,7 @@
         grid=(steps,),
         out_shape=jax.ShapeDtypeStruct(stem.shape, stem.dtype),
         in_specs=[
-            whole(rows, depth),
-            whole(around, depth),
+            whole(*halo.shape),
             whole(around, 1),
             columns(0),
             columns(1),
@@ -440,7 +452,7 @@
         out_specs=piece,
         scratch_shapes=[pltpu.VMEM((around, depth), jnp.bfloat16)],
         name="encode",
-    )(own, halo, exists, weight, weight, weight, bias, stem)
+    )(halo, exists, weight, weight, weight, bias, stem)
 
 
 def layer_norm(block, gain):
@@ -475,28 +487,29 @@
     depth, columns = qkv_weight.shape
     padded = depth + 1 + (-(depth + 1) % 8)
     spread_at = (jnp.arange(width) // depth) * padded + jnp.arange(width) % depth
-    spread = (spread_at[:, None] == jnp.arange(n_tm * padded)[None, :]).astype(jnp.bfloat16)
-    own = jnp.dot(
-        layer_norm(stem, norm_gain), spread, preferred_element_type=jnp.float32
-    ).astype(jnp.bfloat16)
     small = jnp.pad(small, (0, (padded - depth) * columns - cuts[3])).reshape(-1, columns)
-    gathered, halo = gather(jnp.concatenate([qkv_weight, small], axis=0), own, n_tm)
+    gathered, halo = gather(
+        jnp.concatenate([qkv_weight, small], axis=0),
+        stem,
+        norm_gain[None, :],
+        spread_at[:, None],
+        n_tm,
+    )
     weight = gathered.reshape(n_tm * padded, columns)
     small_all = gathered[:, depth]
     all_queries = small_all[:, : cuts[0]].reshape(n_tm * tokens_dev, width)
     all_masks = small_all[:, cuts[0] : cuts[1]].reshape(n_tm * tokens_dev, n_tm)
     seg_low = small_all[:, cuts[1] : cuts[2]].reshape(-1).astype(jnp.int32)
     seg_high = small_all[:, cuts[2] : cuts[3]].reshape(-1).astype(jnp.int32)
-    around = halo.shape[0]
+    around = 4 * REACH + 1
     seg_all = jnp.pad(seg_high * 128 + seg_low, (2 * REACH * rows, 2 * REACH * rows))
-    chip = device // 2
-    seg_wide = lax.dynamic_slice_in_dim(seg_all, chip * 2 * rows, around * rows, 0)
-    block_at = chip * 2 - 2 * REACH + jnp.arange(around, dtype=jnp.int32)
+    seg_wide = lax.dynamic_slice_in_dim(seg_all, device * rows, around * rows, 0)
+    block_at = device - 2 * REACH + jnp.arange(around, dtype=jnp.int32)
     exists = (block_at >= 0) & (block_at < n_tm)
     exists = jnp.repeat(exists.astype(jnp.int32), rows)[:, None]
     same = segment_ids[:, None] == seg_wide[None, :]
     bias = jnp.where(same, jnp.float32(0.0), jnp.float32(-1e30))
-    memory = encode(own, halo.reshape(around * rows, -1), exists, weight, bias, stem)
+    memory = encode(halo.reshape(halo.shape[0] * rows, -1), exists, weight, bias, stem)
     total_tokens = all_queries.shape[0]
     column = lax.dynamic_slice_in_dim(all_masks, device, 1, 1)[:, 0]
     owner = jnp.arange(total_tokens, dtype=jnp.int32) // tokens_dev

time: 175 us -> 173 us (0.989)
  matrix products: 4.57 us -> 0.92 us
  local copies, waits for them, and re-layouts: 10.8 us -> 12.8 us
    dot_general x1 -> x0, matrix products: 3.65 us -> none  [on_device(): jnp.dot(layer_norm(stem, norm_gain), spread, preferred_element_type=jnp.f...]
    reduce_sum x2 -> x0, other arithmetic: 2.31 us -> none  [the longest x1 1.21 us: layer_norm(): var = jnp.mean((values_in - mean) ** 2, axis=-1, keepdims=True)]
where the time goes in v5:
time: 173 us
  Pallas kernels  152 us (88%)
  local copies, waits for them, and re-layouts  12.8 us (7%)
  other arithmetic  6.55 us (4%)
    pallas_call x1, Pallas kernels, gather(): pl.pallas_call(functools.partial(gather_kernel, nx), out_shape=(jax.Shape...  90.6 us
    pallas_call x1, Pallas kernels, deal(): pl.pallas_call(functools.partial(deal_kernel, n), out_shape=jax.ShapeDtyp...  35.7 us
    pallas_call x1, Pallas kernels, encode(): pl.pallas_call(functools.partial(encode_kernel, heads_step), grid=(steps,...  25.3 us

profile of v5, /device:TPU:1, one launch (start us, length us, event | category | flops | bytes accessed | tf_op | source)
XLA Modules:
  0.0 172.7 jit_solution(2566366205820281766)
XLA Ops:
  0.6 0.7 fusion.42
  1.3 0.7 reshape.254
  2.0 0.7 convert_element_type.43
  2.7 0.1 reshape.255
  2.8 1.6 pad_maximum_fusion.w_ref
  4.4 1.1 fusion.12.at_ref
  5.6 1.3 broadcast_in_dim.54.gain_ref
  6.9 90.6 %gather.1 = (bf16[64,24,3840]{2,1,0:T(8,128)(2,1)}, bf16[10,128,1536]{2,1,0:T(8,128)(2,1)}) custom-call(bf16[24,3840]{1,0:T(8,128)(2,1)} %pad_maximum_fusion.w_ref, bf16[128,1280]{1,0:T(8,128)(2,1)} %stem_ref.3, f32[1,1280]{1,0:T(1,128)} %broadcast_in_dim.54.gain_ref, s32[1280,1]{1,0:T(8,128)} %fusion.12.at_ref), custom_call_target="tpu_custom_call" | custom-call | tf_op jit(solution)/shard_map/gather/pallas_call | solution.py:306
  97.5 0.0 copy-start
  97.5 3.1 %slice.33 = bf16[64,1,3840]{2,1,0:T(2,128)(2,1)S(1)} slice(bf16[64,24,3840]{2,1,0:T(8,128)(2,1)} %get-tuple-element.5), slice={[0:64], [20:21], [0:3840]} | slice | bytes 983040 | tf_op jit(solution)/shard_map/slice | solution.py:499
  100.7 0.1 copy.66
  100.7 0.1 pad_dynamic-slice_fusion
  100.8 0.0 copy-done
  100.8 0.9 compare_select_fusion.bias_ref
  101.8 0.1 broadcast_bitcast_fusion
  101.9 1.1 copy.55
  102.9 25.3 %encode.1 = bf16[128,1280]{1,0:T(8,128)(2,1)} custom-call(bf16[1280,1536]{1,0:T(8,128)(2,1)} %bitcast.69, s32[1152,1]{1,0:T(8,128)} %bitcast.74, bf16[1536,3840]{1,0:T(8,128)(2,1)} %bitcast.66, bf16[1536,3840]{1,0:T(8,128)(2,1)} %bitcast.67, bf16[1536,3840]{1,0:T(8,128)(2,1)} %bitcast.68, f32[128,1152]{1,0:T(8,128)} %compare_select_fusion.bias_ref, ...), custom_call_target="tpu_custom_call" | custom-call | tf_op jit(solution)/shard_map/encode/pallas_call | solution.py:439
  128.2 1.2 copy.37
  129.4 0.6 reshape_reshape.3
  130.1 0.6 fusion.46
  130.7 0.1 reshape.260
  130.8 0.2 compare_reduce_fusion
  131.0 0.3 fusion.4
  131.3 0.4 copy.40
  131.7 0.5 reshape.261
  132.2 0.2 fusion.5
  132.5 0.1 maximum_bitcast_fusion
  132.6 0.2 copy.45
  132.8 0.1 reshape.262
  132.9 0.8 copy.56
  133.7 35.7 %deal.1 = bf16[64,24,128]{2,1,0:T(8,128)(2,1)} custom-call(bf16[64,24,128]{2,1,0:T(8,128)(2,1)} %bitcast.75), custom_call_target="tpu_custom_call" | custom-call | tf_op jit(solution)/shard_map/deal/pallas_call | solution.py:376
  169.4 1.0 copy.65
  170.5 0.1 copy.46
  170.6 0.1 fusion.41
  170.7 0.2 fusion.31
  170.9 0.1 copy.49
  171.0 0.5 mul.50
  171.4 0.4 mul.51
  171.8 0.1 fusion.15
  171.9 0.1 div.46
  172.0 0.1 div.47
  172.1 0.6 divide_convert_fusion
  (19 shorter events, 0.2 us)
Async XLA Ops:
  97.5 3.3 %copy-start = (s32[128]{0:T(128)S(1)}, s32[128]{0:T(128)}, u32[]{:S(2)}) copy-start(s32[128]{0:T(128)} %param.9) | copy-start | bytes 1540

commit v6 on v5

--- a/solution.py
+++ b/solution.py
@@ -13,7 +13,7 @@
 MESH = pl.DeviceIdType.MESH
 
 
-def gather_kernel(nx, w_ref, stem_ref, gain_ref, at_ref, wide_ref, halo_ref, own_ref, w_recv, w_zs, w_xs, w_ps, h_recv, h_zs, h_ps, own_sem):
+def gather_kernel(nx, depth, w_ref, stem_ref, gain_ref, wide_ref, halo_ref, own_ref, w_recv, w_zs, w_xs, w_ps, h_recv, h_zs, h_ps, own_sem):
     me = lax.axis_index("tm")
     core = lax.rem(me, 2)
     chip = me // 2
@@ -120,8 +120,11 @@
     own_h = pltpu.make_async_copy(own_ref, halo_ref.at[own_slot], own_sem.at[1])
     own_w.start()
 
-    lanes = lax.broadcasted_iota(jnp.int32, (at_ref.shape[0], own_ref.shape[1]), 1)
-    spread = jnp.where(lanes == at_ref[...], 1.0, 0.0).astype(jnp.bfloat16)
+    width = stem_ref.shape[1]
+    source = lax.broadcasted_iota(jnp.int32, (width, 1), 0)
+    shard = lax.shift_right_logical(source * (2**20 // depth + 1), 20)
+    lanes = lax.broadcasted_iota(jnp.int32, (width, own_ref.shape[1]), 1)
+    spread = jnp.where(lanes == source + shard * (w_ref.shape[0] - depth), 1.0, 0.0).astype(jnp.bfloat16)
     own_ref[...] = jnp.dot(
         layer_norm(stem_ref[...], gain_ref[...]), spread, preferred_element_type=jnp.float32
     ).astype(jnp.bfloat16)
@@ -299,17 +302,17 @@
     own_h.wait()
 
 
-def gather(wide, stem, gain, spread_at, n_tm):
+def gather(wide, depth, stem, gain, n_tm):
     nx = n_tm // (2 * NZ)
     own = (stem.shape[0], n_tm * wide.shape[0])
     dma = pltpu.SemaphoreType.DMA
     return pl.pallas_call(
-        functools.partial(gather_kernel, nx),
+        functools.partial(gather_kernel, nx, depth),
         out_shape=(
             jax.ShapeDtypeStruct((n_tm, *wide.shape), wide.dtype),
             jax.ShapeDtypeStruct((4 * REACH + 2, *own), stem.dtype),
         ),
-        in_specs=[pl.BlockSpec(memory_space=pltpu.VMEM)] * 4,
+        in_specs=[pl.BlockSpec(memory_space=pltpu.VMEM)] * 3,
         out_specs=(pl.BlockSpec(memory_space=pl.ANY), pl.BlockSpec(memory_space=pl.ANY)),
         scratch_shapes=[
             pltpu.VMEM(own, stem.dtype),
@@ -324,7 +327,7 @@
         ],
         compiler_params=pltpu.CompilerParams(collective_id=0, has_side_effects=True),
         name="gather",
-    )(wide, stem, gain, spread_at)
+    )(wide, stem, gain)
 
 
 def deal_kernel(n, out_ref, in_ref, send_sem, recv_sem, own_sem):
@@ -384,14 +387,17 @@
     )(payload)
 
 
-def encode_kernel(heads_step, halo_ref, exists_ref, wq_ref, wk_ref, wv_ref, bias_ref, stem_ref, out_ref, clean):
+def encode_kernel(heads_step, halo_ref, wq_ref, wk_ref, wv_ref, bias_ref, stem_ref, out_ref, clean):
     rows = out_ref.shape[0]
 
     @pl.when(pl.program_id(0) == 0)
     def _():
-        first = lax.rem(lax.axis_index("tm"), 2) * rows
+        me = lax.axis_index("tm")
+        first = lax.rem(me, 2) * rows
         near = halo_ref[pl.ds(pl.multiple_of(first, rows), clean.shape[0]), :]
-        clean[...] = jnp.where(exists_ref[...] > 0, near, jnp.bfloat16(0))
+        place = lax.broadcasted_iota(jnp.int32, near.shape, 0) + (me - 2 * REACH) * rows
+        exists = (place >= 0) & (place < lax.axis_size("tm") * rows)
+        clean[...] = jnp.where(exists, near, jnp.bfloat16(0))
 
     def project(block, w_ref):
         return jnp.dot(block, w_ref[...], preferred_element_type=jnp.float32).astype(jnp.bfloat16)
@@ -421,7 +427,7 @@
         out_ref[:, at] = (stem_ref[:, at].astype(jnp.float32) + context).astype(jnp.bfloat16)
 
 
-def encode(halo, exists, weight, bias, stem):
+def encode(halo, weight, bias, stem):
     rows, width = stem.shape
     depth = halo.shape[1]
     around = bias.shape[1]
@@ -442,7 +448,6 @@
         out_shape=jax.ShapeDtypeStruct(stem.shape, stem.dtype),
         in_specs=[
             whole(*halo.shape),
-            whole(around, 1),
             columns(0),
             columns(1),
             columns(2),
@@ -452,7 +457,7 @@
         out_specs=piece,
         scratch_shapes=[pltpu.VMEM((around, depth), jnp.bfloat16)],
         name="encode",
-    )(halo, exists, weight, weight, weight, bias, stem)
+    )(halo, weight, weight, weight, bias, stem)
 
 
 def layer_norm(block, gain):
@@ -486,13 +491,12 @@
     cuts += [cuts[1] + rows, cuts[1] + 2 * rows]
     depth, columns = qkv_weight.shape
     padded = depth + 1 + (-(depth + 1) % 8)
-    spread_at = (jnp.arange(width) // depth) * padded + jnp.arange(width) % depth
     small = jnp.pad(small, (0, (padded - depth) * columns - cuts[3])).reshape(-1, columns)
     gathered, halo = gather(
         jnp.concatenate([qkv_weight, small], axis=0),
+        depth,
         stem,
         norm_gain[None, :],
-        spread_at[:, None],
         n_tm,
     )
     weight = gathered.reshape(n_tm * padded, columns)
@@ -504,12 +508,9 @@
     around = 4 * REACH + 1
     seg_all = jnp.pad(seg_high * 128 + seg_low, (2 * REACH * rows, 2 * REACH * rows))
     seg_wide = lax.dynamic_slice_in_dim(seg_all, device * rows, around * rows, 0)
-    block_at = device - 2 * REACH + jnp.arange(around, dtype=jnp.int32)
-    exists = (block_at >= 0) & (block_at < n_tm)
-    exists = jnp.repeat(exists.astype(jnp.int32), rows)[:, None]
     same = segment_ids[:, None] == seg_wide[None, :]
     bias = jnp.where(same, jnp.float32(0.0), jnp.float32(-1e30))
-    memory = encode(halo.reshape(halo.shape[0] * rows, -1), exists, weight, bias, stem)
+    memory = encode(halo.reshape(halo.shape[0] * rows, -1), weight, bias, stem)
     total_tokens = all_queries.shape[0]
     column = lax.dynamic_slice_in_dim(all_masks, device, 1, 1)[:, 0]
     owner = jnp.arange(total_tokens, dtype=jnp.int32) // tokens_dev

time: 173 us -> 170 us (0.983)
  no operation moved by 1% of the time
where the time goes in v6:
time: 170 us
  Pallas kernels  151 us (89%)
  local copies, waits for them, and re-layouts  11.6 us (7%)
  other arithmetic  5.41 us (3%)
    pallas_call x1, Pallas kernels, gather(): pl.pallas_call(functools.partial(gather_kernel, nx, depth), out_shape=(ja...  90.4 us
    pallas_call x1, Pallas kernels, deal(): pl.pallas_call(functools.partial(deal_kernel, n), out_shape=jax.ShapeDtyp...  35.7 us
    pallas_call x1, Pallas kernels, encode(): pl.pallas_call(functools.partial(encode_kernel, heads_step), grid=(steps,...  25.1 us

profile of v6, /device:TPU:1, one launch (start us, length us, event | category | flops | bytes accessed | tf_op | source)
XLA Modules:
  0.0 169.9 jit_solution(12075466903338726033)
XLA Ops:
  0.6 0.7 fusion.33
  1.3 0.7 convert_element_type.40
  2.0 0.1 reshape.202
  2.1 0.7 reshape.201
  2.8 1.6 pad_maximum_fusion.w_ref
  4.4 1.3 broadcast_in_dim.50.gain_ref
  5.7 90.4 %gather.1 = (bf16[64,24,3840]{2,1,0:T(8,128)(2,1)}, bf16[10,128,1536]{2,1,0:T(8,128)(2,1)}) custom-call(bf16[24,3840]{1,0:T(8,128)(2,1)} %pad_maximum_fusion.w_ref, bf16[128,1280]{1,0:T(8,128)(2,1)} %stem_ref.3, f32[1,1280]{1,0:T(1,128)} %broadcast_in_dim.50.gain_ref), custom_call_target="tpu_custom_call" | custom-call | tf_op jit(solution)/shard_map/gather/pallas_call | solution.py:309
  96.1 0.0 copy-start
  96.1 3.1 %slice.33 = bf16[64,1,3840]{2,1,0:T(2,128)(2,1)S(1)} slice(bf16[64,24,3840]{2,1,0:T(8,128)(2,1)} %get-tuple-element.5), slice={[0:64], [20:21], [0:3840]} | slice | bytes 983040 | tf_op jit(solution)/shard_map/slice | solution.py:503
  99.3 0.1 copy.60
  99.3 0.1 pad_dynamic-slice_fusion
  99.4 0.0 copy-done
  99.4 0.9 compare_select_fusion.bias_ref
  100.4 25.1 %encode.1 = bf16[128,1280]{1,0:T(8,128)(2,1)} custom-call(bf16[1280,1536]{1,0:T(8,128)(2,1)} %bitcast.62, bf16[1536,3840]{1,0:T(8,128)(2,1)} %bitcast.59, bf16[1536,3840]{1,0:T(8,128)(2,1)} %bitcast.60, bf16[1536,3840]{1,0:T(8,128)(2,1)} %bitcast.61, f32[128,1152]{1,0:T(8,128)} %compare_select_fusion.bias_ref, bf16[128,1280]{1,0:T(8,128)(2,1)} %stem_ref.3), custom_call_target="tpu_custom_call" | custom-call | tf_op jit(solution)/shard_map/encode/pallas_call | solution.py:445
  125.4 1.2 copy.34
  126.7 0.6 reshape_reshape.3
  127.3 0.6 fusion.37
  127.9 0.1 reshape.207
  128.0 0.2 compare_reduce_fusion
  128.2 0.2 fusion.1
  128.5 0.1 maximum_bitcast_fusion
  128.6 0.2 copy.42
  128.8 0.1 reshape.209
  128.9 0.3 fusion
  129.2 0.4 copy.37
  129.7 0.5 reshape.208
  130.2 0.8 copy.51
  131.0 35.7 %deal.1 = bf16[64,24,128]{2,1,0:T(8,128)(2,1)} custom-call(bf16[64,24,128]{2,1,0:T(8,128)(2,1)} %bitcast.67), custom_call_target="tpu_custom_call" | custom-call | tf_op jit(solution)/shard_map/deal/pallas_call | solution.py:379
  166.6 1.0 copy.59
  167.7 0.1 copy.43
  167.8 0.1 fusion.32
  167.9 0.2 fusion.22
  168.1 0.1 copy.46
  168.2 0.5 mul.35
  168.7 0.4 mul.36
  169.1 0.1 fusion.6
  169.2 0.1 div.32
  169.2 0.1 div.33
  169.3 0.6 divide_convert_fusion
  (17 shorter events, 0.2 us)
Async XLA Ops:
  96.1 3.3 %copy-start = (s32[128]{0:T(128)S(1)}, s32[128]{0:T(128)}, u32[]{:S(2)}) copy-start(s32[128]{0:T(128)} %param.9) | copy-start | bytes 1540
